TPU v7x, 128 devices: a whole 4x4x4 slice. The times are simulated.
128 devices in a mesh: rows: 128 (over y, x, z, core).
Axes of the slice: x: 4, y: 4, z: 4, core: 2. Of those that a mesh axis runs over, the one named last changes fastest.
Arguments:
- tracers_init: float32 [65536, 256], P('rows'), may hold values from -6 to 6
- source: float32 [65536, 256], P('rows'), may hold values from -4 to 4
- explicit_tiles: float32 [512, 8, 128, 128], P('rows'), may hold values from -0.0625 to 0.0625
- implicit_tiles: float32 [512, 8, 128, 128], P('rows'), may hold values from -0.0625 to 0.0625
- explicit_cols: int32 [512, 8], P('rows'), may hold values from 0 to 6, as said below
- implicit_cols: int32 [512, 8], P('rows'), may hold values from 0 to 6, as said below
- send_rows: int32 [1024, 48], P('rows'), may hold values from 0 to 511
Outputs:
- tracers: float32 [65536, 256], P('rows')
Inputs may be any that keep to these rules, and one draw needn't show every extreme that they name: `explicit_cols`: each entry names one of the 7 blocks of the device's own rows followed by its halo rows. `implicit_cols`: each entry names one of the 7 blocks of the device's own rows followed by its halo rows. `send_rows`: local row numbers of the sending device.
All inputs are finite; a program needn't handle non-finite values.
Results may differ from a plain program's by a relative error of at most 0.0001.
Values sent between devices are 32-bit elements; how exact they have to be, the bound alone decides.
A program may use at most 64 MiB of HBM per device.

v0:
```python
import jax
import jax.numpy as jnp
from jax import lax
from jax.sharding import PartitionSpec as P

STEPS = 3


def from_behind(x, axis, by):
    devices = lax.axis_size(axis)
    return lax.ppermute(x, axis, [(i, (i + by) % devices) for i in range(devices)])


def partner_offset(offset_index):
    return (offset_index // 2 + 1) * (1 if offset_index % 2 == 0 else -1)


def on_device(
    tracers_init, source, explicit_tiles, implicit_tiles, explicit_cols, implicit_cols, send_rows
):
    local_rows, panels = tracers_init.shape
    block_rows = explicit_tiles.shape[2]
    block_count = explicit_tiles.shape[0]
    slot_count = explicit_tiles.shape[1]
    partners = send_rows.shape[0]
    halo_size = send_rows.shape[1]
    halo_blocks = partners * halo_size // block_rows

    def gather_halo(state):
        payloads = state[send_rows]
        pieces = []
        for offset_index in range(partners):
            pieces.append(from_behind(payloads[offset_index], "rows", partner_offset(offset_index)))
        return jnp.concatenate(pieces, axis=0)

    def apply(tiles, columns, state):
        halo = gather_halo(state)
        total = state.reshape(block_count, block_rows, panels)
        own_blocks = total
        for slot_index in range(slot_count):
            column = columns[:, slot_index]
            inside = column < block_count
            picked = own_blocks[jnp.minimum(column, block_count - 1)]
            weights = jnp.where(inside[:, None, None], tiles[:, slot_index], 0.0)
            total = total + jnp.einsum(
                "rij,rjp->rip", weights, picked, precision=lax.Precision.HIGHEST
            )
        targets = block_count + jnp.arange(halo_blocks, dtype=jnp.int32)
        selector = (columns[:, :, None] == targets[None, None, :]).astype(jnp.float32)
        merged = jnp.einsum("rkh,rkij->rhij", selector, tiles, precision=lax.Precision.HIGHEST)
        halo_view = halo.reshape(halo_blocks, block_rows, panels)
        total = total + jnp.einsum(
            "rhij,hjp->rip", merged, halo_view, precision=lax.Precision.HIGHEST
        )
        return total.reshape(local_rows, panels)

    tracers = tracers_init
    for repeat in range(STEPS):
        middle = apply(explicit_tiles, explicit_cols, tracers) + source
        tracers = apply(implicit_tiles, implicit_cols, middle)
    return tracers


def solution(mesh):
    return jax.shard_map(
        on_device,
        mesh=mesh,
        in_specs=(
            P("rows", None),
            P("rows", None),
            P("rows", None, None, None),
            P("rows", None, None, None),
            P("rows", None),
            P("rows", None),
            P("rows", None),
        ),
        out_specs=P("rows", None),
        check_vma=False,
    )
```

profile of v0, /device:TPU:0, one launch (start us, length us, event | category | flops | bytes accessed | tf_op | source)
XLA Modules:
  0.0 342.4 jit_solution(17393182443997516106)
XLA Ops:
  0.8 2.8 gather_fusion.8
  4.2 8.2 %collective-permute-start.1 = (f32[48,256]{1,0:T(8,128)S(1)}, f32[48,256]{1,0:T(8,128)}, u32[]{:S(2)}, u32[]{:S(2)}) collective-permute-start(f32[48,256]{1,0:T(8,128)S(1)} %get-tuple-element.83), channel_id=1, source_target_pairs={{0,127},{1,0},{2,1},{3,2},{4,3},{5,4},{6,5},{7,6},{8,7},{9,8},{10,... | collective-permute-start | bytes 147464 | tf_op jit(solution)/shard_map/ppermute | solution.py:11
  12.5 7.5 %collective-permute-start.3 = (f32[48,256]{1,0:T(8,128)S(1)}, f32[48,256]{1,0:T(8,128)}, u32[]{:S(2)}, u32[]{:S(2)}) collective-permute-start(f32[48,256]{1,0:T(8,128)S(1)} %get-tuple-element.81), channel_id=1, source_target_pairs={{0,126},{1,127},{2,0},{3,1},{4,2},{5,3},{6,4},{7,5},{8,6},{9,7},{1... | collective-permute-start | bytes 147464 | tf_op jit(solution)/shard_map/ppermute | solution.py:11
  35.5 3.0 fusion.2
  38.6 3.2 fusion
  49.7 7.4 %collective-permute-start.5 = (f32[48,256]{1,0:T(8,128)S(1)}, f32[48,256]{1,0:T(8,128)S(1)}, u32[]{:S(2)}, u32[]{:S(2)}) collective-permute-start(f32[48,256]{1,0:T(8,128)S(1)} %get-tuple-element.79), channel_id=1, source_target_pairs={{0,125},{1,126},{2,127},{3,0},{4,1},{5,2},{6,3},{7,4},{8,5},{9,6},... | collective-permute-start | bytes 147464 | tf_op jit(solution)/shard_map/ppermute | solution.py:11
  58.8 7.9 %collective-permute-start.7 = (f32[48,256]{1,0:T(8,128)S(1)}, f32[48,256]{1,0:T(8,128)S(1)}, u32[]{:S(2)}, u32[]{:S(2)}) collective-permute-start(f32[48,256]{1,0:T(8,128)S(1)} %get-tuple-element.77), channel_id=1, source_target_pairs={{0,124},{1,125},{2,126},{3,127},{4,0},{5,1},{6,2},{7,3},{8,4},{9,5... | collective-permute-start | bytes 147464 | tf_op jit(solution)/shard_map/ppermute | solution.py:11
  70.3 1.7 gather_fusion.17
  84.1 7.2 %collective-permute-start.9 = (f32[48,256]{1,0:T(8,128)S(1)}, f32[48,256]{1,0:T(8,128)S(1)}, u32[]{:S(2)}, u32[]{:S(2)}) collective-permute-start(f32[48,256]{1,0:T(8,128)S(1)} %get-tuple-element.75), channel_id=1, source_target_pairs={{0,127},{1,0},{2,1},{3,2},{4,3},{5,4},{6,5},{7,6},{8,7},{9,8},{10,... | collective-permute-start | bytes 147464 | tf_op jit(solution)/shard_map/ppermute | solution.py:11
  91.3 7.5 %collective-permute-start.11 = (f32[48,256]{1,0:T(8,128)S(1)}, f32[48,256]{1,0:T(8,128)S(1)}, u32[]{:S(2)}, u32[]{:S(2)}) collective-permute-start(f32[48,256]{1,0:T(8,128)S(1)} %get-tuple-element.73), channel_id=1, source_target_pairs={{0,126},{1,127},{2,0},{3,1},{4,2},{5,3},{6,4},{7,5},{8,6},{9,7},{1... | collective-permute-start | bytes 147464 | tf_op jit(solution)/shard_map/ppermute | solution.py:11
  98.7 1.8 convolution_add_fusion.39
  100.5 1.7 convolution_add_fusion.38
  106.3 7.5 %collective-permute-start.13 = (f32[48,256]{1,0:T(8,128)S(1)}, f32[48,256]{1,0:T(8,128)S(1)}, u32[]{:S(2)}, u32[]{:S(2)}) collective-permute-start(f32[48,256]{1,0:T(8,128)S(1)} %get-tuple-element.71), channel_id=1, source_target_pairs={{0,125},{1,126},{2,127},{3,0},{4,1},{5,2},{6,3},{7,4},{8,5},{9,6},... | collective-permute-start | bytes 147464 | tf_op jit(solution)/shard_map/ppermute | solution.py:11
  114.0 8.2 %collective-permute-start.15 = (f32[48,256]{1,0:T(8,128)S(1)}, f32[48,256]{1,0:T(8,128)S(1)}, u32[]{:S(2)}, u32[]{:S(2)}) collective-permute-start(f32[48,256]{1,0:T(8,128)S(1)} %get-tuple-element.69), channel_id=1, source_target_pairs={{0,124},{1,125},{2,126},{3,127},{4,0},{5,1},{6,2},{7,3},{8,4},{9,5... | collective-permute-start | bytes 147464 | tf_op jit(solution)/shard_map/ppermute | solution.py:11
  137.1 2.5 convolution_add_fusion.31
  139.6 1.7 gather_fusion.26
  141.4 7.2 %collective-permute-start.17 = (f32[48,256]{1,0:T(8,128)S(1)}, f32[48,256]{1,0:T(8,128)S(1)}, u32[]{:S(2)}, u32[]{:S(2)}) collective-permute-start(f32[48,256]{1,0:T(8,128)S(1)} %get-tuple-element.67), channel_id=1, source_target_pairs={{0,127},{1,0},{2,1},{3,2},{4,3},{5,4},{6,5},{7,6},{8,7},{9,8},{10,... | collective-permute-start | bytes 147464 | tf_op jit(solution)/shard_map/ppermute | solution.py:11
  148.6 7.5 %collective-permute-start.19 = (f32[48,256]{1,0:T(8,128)S(1)}, f32[48,256]{1,0:T(8,128)S(1)}, u32[]{:S(2)}, u32[]{:S(2)}) collective-permute-start(f32[48,256]{1,0:T(8,128)S(1)} %get-tuple-element.65), channel_id=1, source_target_pairs={{0,126},{1,127},{2,0},{3,1},{4,2},{5,3},{6,4},{7,5},{8,6},{9,7},{1... | collective-permute-start | bytes 147464 | tf_op jit(solution)/shard_map/ppermute | solution.py:11
  156.0 1.8 convolution_add_fusion.30
  162.0 7.5 %collective-permute-start.21 = (f32[48,256]{1,0:T(8,128)S(1)}, f32[48,256]{1,0:T(8,128)S(1)}, u32[]{:S(2)}, u32[]{:S(2)}) collective-permute-start(f32[48,256]{1,0:T(8,128)S(1)} %get-tuple-element.63), channel_id=1, source_target_pairs={{0,125},{1,126},{2,127},{3,0},{4,1},{5,2},{6,3},{7,4},{8,5},{9,6},... | collective-permute-start | bytes 147464 | tf_op jit(solution)/shard_map/ppermute | solution.py:11
  169.6 8.0 %collective-permute-start.23 = (f32[48,256]{1,0:T(8,128)S(1)}, f32[48,256]{1,0:T(8,128)S(1)}, u32[]{:S(2)}, u32[]{:S(2)}) collective-permute-start(f32[48,256]{1,0:T(8,128)S(1)} %get-tuple-element.61), channel_id=1, source_target_pairs={{0,124},{1,125},{2,126},{3,127},{4,0},{5,1},{6,2},{7,3},{8,4},{9,5... | collective-permute-start | bytes 147464 | tf_op jit(solution)/shard_map/ppermute | solution.py:11
  177.7 1.7 collective-permute-done.22
  192.6 1.7 gather_fusion.35
  194.3 1.9 convolution_add_fusion.23
  196.3 7.2 %collective-permute-start.25 = (f32[48,256]{1,0:T(8,128)S(1)}, f32[48,256]{1,0:T(8,128)S(1)}, u32[]{:S(2)}, u32[]{:S(2)}) collective-permute-start(f32[48,256]{1,0:T(8,128)S(1)} %get-tuple-element.59), channel_id=1, source_target_pairs={{0,127},{1,0},{2,1},{3,2},{4,3},{5,4},{6,5},{7,6},{8,7},{9,8},{10,... | collective-permute-start | bytes 147464 | tf_op jit(solution)/shard_map/ppermute | solution.py:11
  203.5 7.5 %collective-permute-start.27 = (f32[48,256]{1,0:T(8,128)S(1)}, f32[48,256]{1,0:T(8,128)S(1)}, u32[]{:S(2)}, u32[]{:S(2)}) collective-permute-start(f32[48,256]{1,0:T(8,128)S(1)} %get-tuple-element.57), channel_id=1, source_target_pairs={{0,126},{1,127},{2,0},{3,1},{4,2},{5,3},{6,4},{7,5},{8,6},{9,7},{1... | collective-permute-start | bytes 147464 | tf_op jit(solution)/shard_map/ppermute | solution.py:11
  211.0 1.7 convolution_add_fusion.22
  216.7 7.5 %collective-permute-start.29 = (f32[48,256]{1,0:T(8,128)S(1)}, f32[48,256]{1,0:T(8,128)S(1)}, u32[]{:S(2)}, u32[]{:S(2)}) collective-permute-start(f32[48,256]{1,0:T(8,128)S(1)} %get-tuple-element.55), channel_id=1, source_target_pairs={{0,125},{1,126},{2,127},{3,0},{4,1},{5,2},{6,3},{7,4},{8,5},{9,6},... | collective-permute-start | bytes 147464 | tf_op jit(solution)/shard_map/ppermute | solution.py:11
  224.3 8.0 %collective-permute-start.31 = (f32[48,256]{1,0:T(8,128)S(1)}, f32[48,256]{1,0:T(8,128)S(1)}, u32[]{:S(2)}, u32[]{:S(2)}) collective-permute-start(f32[48,256]{1,0:T(8,128)S(1)} %get-tuple-element.53), channel_id=1, source_target_pairs={{0,124},{1,125},{2,126},{3,127},{4,0},{5,1},{6,2},{7,3},{8,4},{9,5... | collective-permute-start | bytes 147464 | tf_op jit(solution)/shard_map/ppermute | solution.py:11
  232.4 1.7 collective-permute-done.30
  241.2 1.6 gather_fusion.40
  247.3 2.5 convolution_add_fusion.15
  249.8 1.7 gather_fusion.44
  251.6 7.2 %collective-permute-start.33 = (f32[48,256]{1,0:T(8,128)S(1)}, f32[48,256]{1,0:T(8,128)S(1)}, u32[]{:S(2)}, u32[]{:S(2)}) collective-permute-start(f32[48,256]{1,0:T(8,128)S(1)} %get-tuple-element.51), channel_id=1, source_target_pairs={{0,127},{1,0},{2,1},{3,2},{4,3},{5,4},{6,5},{7,6},{8,7},{9,8},{10,... | collective-permute-start | bytes 147464 | tf_op jit(solution)/shard_map/ppermute | solution.py:11
  258.8 7.5 %collective-permute-start.35 = (f32[48,256]{1,0:T(8,128)S(1)}, f32[48,256]{1,0:T(8,128)S(1)}, u32[]{:S(2)}, u32[]{:S(2)}) collective-permute-start(f32[48,256]{1,0:T(8,128)S(1)} %get-tuple-element.49), channel_id=1, source_target_pairs={{0,126},{1,127},{2,0},{3,1},{4,2},{5,3},{6,4},{7,5},{8,6},{9,7},{1... | collective-permute-start | bytes 147464 | tf_op jit(solution)/shard_map/ppermute | solution.py:11
  266.3 1.8 convolution_add_fusion.14
  272.2 7.5 %collective-permute-start.37 = (f32[48,256]{1,0:T(8,128)S(1)}, f32[48,256]{1,0:T(8,128)S(1)}, u32[]{:S(2)}, u32[]{:S(2)}) collective-permute-start(f32[48,256]{1,0:T(8,128)S(1)} %get-tuple-element.47), channel_id=1, source_target_pairs={{0,125},{1,126},{2,127},{3,0},{4,1},{5,2},{6,3},{7,4},{8,5},{9,6},... | collective-permute-start | bytes 147464 | tf_op jit(solution)/shard_map/ppermute | solution.py:11
  279.9 8.0 %collective-permute-start.39 = (f32[48,256]{1,0:T(8,128)S(1)}, f32[48,256]{1,0:T(8,128)S(1)}, u32[]{:S(2)}, u32[]{:S(2)}) collective-permute-start(f32[48,256]{1,0:T(8,128)S(1)} %get-tuple-element.45), channel_id=1, source_target_pairs={{0,124},{1,125},{2,126},{3,127},{4,0},{5,1},{6,2},{7,3},{8,4},{9,5... | collective-permute-start | bytes 147464 | tf_op jit(solution)/shard_map/ppermute | solution.py:11
  288.0 1.7 collective-permute-done.38
  298.8 1.7 gather_fusion.53
  300.6 1.9 convolution_add_fusion.7
  302.6 7.2 %collective-permute-start.41 = (f32[48,256]{1,0:T(8,128)S(1)}, f32[48,256]{1,0:T(8,128)S(1)}, u32[]{:S(2)}, u32[]{:S(2)}) collective-permute-start(f32[48,256]{1,0:T(8,128)S(1)} %get-tuple-element.43), channel_id=1, source_target_pairs={{0,127},{1,0},{2,1},{3,2},{4,3},{5,4},{6,5},{7,6},{8,7},{9,8},{10,... | collective-permute-start | bytes 147464 | tf_op jit(solution)/shard_map/ppermute | solution.py:11
  309.8 7.5 %collective-permute-start.43 = (f32[48,256]{1,0:T(8,128)S(1)}, f32[48,256]{1,0:T(8,128)S(1)}, u32[]{:S(2)}, u32[]{:S(2)}) collective-permute-start(f32[48,256]{1,0:T(8,128)S(1)} %get-tuple-element.41), channel_id=1, source_target_pairs={{0,126},{1,127},{2,0},{3,1},{4,2},{5,3},{6,4},{7,5},{8,6},{9,7},{1... | collective-permute-start | bytes 147464 | tf_op jit(solution)/shard_map/ppermute | solution.py:11
  317.3 1.7 convolution_add_fusion.6
  322.9 7.5 %collective-permute-start.45 = (f32[48,256]{1,0:T(8,128)S(1)}, f32[48,256]{1,0:T(8,128)S(1)}, u32[]{:S(2)}, u32[]{:S(2)}) collective-permute-start(f32[48,256]{1,0:T(8,128)S(1)} %get-tuple-element.39), channel_id=1, source_target_pairs={{0,125},{1,126},{2,127},{3,0},{4,1},{5,2},{6,3},{7,4},{8,5},{9,6},... | collective-permute-start | bytes 147464 | tf_op jit(solution)/shard_map/ppermute | solution.py:11
  330.6 7.8 %collective-permute-start.47 = (f32[48,256]{1,0:T(8,128)S(1)}, f32[48,256]{1,0:T(8,128)S(1)}, u32[]{:S(2)}, u32[]{:S(2)}) collective-permute-start(f32[48,256]{1,0:T(8,128)S(1)} %get-tuple-element.37), channel_id=1, source_target_pairs={{0,124},{1,125},{2,126},{3,127},{4,0},{5,1},{6,2},{7,3},{8,4},{9,5... | collective-permute-start | bytes 147464 | tf_op jit(solution)/shard_map/ppermute | solution.py:11
  338.4 1.9 collective-permute-done.46
  340.4 1.8 fusion.9
  (421 shorter events, 110.8 us)
Async XLA Ops:
  4.2 45.5 %collective-permute-start = (f32[48,256]{1,0:T(8,128)}, f32[48,256]{1,0:T(8,128)}, u32[]{:S(2)}, u32[]{:S(2)}) collective-permute-start(f32[48,256]{1,0:T(8,128)} %get-tuple-element.84), channel_id=1, source_target_pairs={{0,1},{1,2},{2,3},{3,4},{4,5},{5,6},{6,7},{7,8},{8,9},{9,10},{10,1... | collective-permute-start | bytes 147464 | tf_op jit(solution)/shard_map/ppermute | solution.py:11
  4.2 53.7 %collective-permute-start.1 = (f32[48,256]{1,0:T(8,128)S(1)}, f32[48,256]{1,0:T(8,128)}, u32[]{:S(2)}, u32[]{:S(2)}) collective-permute-start(f32[48,256]{1,0:T(8,128)S(1)} %get-tuple-element.83), channel_id=1, source_target_pairs={{0,127},{1,0},{2,1},{3,2},{4,3},{5,4},{6,5},{7,6},{8,7},{9,8},{10,... | collective-permute-start | bytes 147464 | tf_op jit(solution)/shard_map/ppermute | solution.py:11
  12.5 46.3 %collective-permute-start.2 = (f32[48,256]{1,0:T(8,128)S(1)}, f32[48,256]{1,0:T(8,128)}, u32[]{:S(2)}, u32[]{:S(2)}) collective-permute-start(f32[48,256]{1,0:T(8,128)S(1)} %get-tuple-element.82), channel_id=1, source_target_pairs={{0,2},{1,3},{2,4},{3,5},{4,6},{5,7},{6,8},{7,9},{8,10},{9,11},{10,... | collective-permute-start | bytes 147464 | tf_op jit(solution)/shard_map/ppermute | solution.py:11
  12.5 55.0 %collective-permute-start.3 = (f32[48,256]{1,0:T(8,128)S(1)}, f32[48,256]{1,0:T(8,128)}, u32[]{:S(2)}, u32[]{:S(2)}) collective-permute-start(f32[48,256]{1,0:T(8,128)S(1)} %get-tuple-element.81), channel_id=1, source_target_pairs={{0,126},{1,127},{2,0},{3,1},{4,2},{5,3},{6,4},{7,5},{8,6},{9,7},{1... | collective-permute-start | bytes 147464 | tf_op jit(solution)/shard_map/ppermute | solution.py:11
  19.9 48.4 %collective-permute-start.4 = (f32[48,256]{1,0:T(8,128)S(1)}, f32[48,256]{1,0:T(8,128)}, u32[]{:S(2)}, u32[]{:S(2)}) collective-permute-start(f32[48,256]{1,0:T(8,128)S(1)} %get-tuple-element.80), channel_id=1, source_target_pairs={{0,3},{1,4},{2,5},{3,6},{4,7},{5,8},{6,9},{7,10},{8,11},{9,12},{10... | collective-permute-start | bytes 147464 | tf_op jit(solution)/shard_map/ppermute | solution.py:11
  49.7 19.4 %collective-permute-start.5 = (f32[48,256]{1,0:T(8,128)S(1)}, f32[48,256]{1,0:T(8,128)S(1)}, u32[]{:S(2)}, u32[]{:S(2)}) collective-permute-start(f32[48,256]{1,0:T(8,128)S(1)} %get-tuple-element.79), channel_id=1, source_target_pairs={{0,125},{1,126},{2,127},{3,0},{4,1},{5,2},{6,3},{7,4},{8,5},{9,6},... | collective-permute-start | bytes 147464 | tf_op jit(solution)/shard_map/ppermute | solution.py:11
  58.0 11.2 %collective-permute-start.6 = (f32[48,256]{1,0:T(8,128)S(1)}, f32[48,256]{1,0:T(8,128)S(1)}, u32[]{:S(2)}, u32[]{:S(2)}) collective-permute-start(f32[48,256]{1,0:T(8,128)S(1)} %get-tuple-element.78), channel_id=1, source_target_pairs={{0,4},{1,5},{2,6},{3,7},{4,8},{5,9},{6,10},{7,11},{8,12},{9,13},{1... | collective-permute-start | bytes 147464 | tf_op jit(solution)/shard_map/ppermute | solution.py:11
  58.8 10.4 %collective-permute-start.7 = (f32[48,256]{1,0:T(8,128)S(1)}, f32[48,256]{1,0:T(8,128)S(1)}, u32[]{:S(2)}, u32[]{:S(2)}) collective-permute-start(f32[48,256]{1,0:T(8,128)S(1)} %get-tuple-element.77), channel_id=1, source_target_pairs={{0,124},{1,125},{2,126},{3,127},{4,0},{5,1},{6,2},{7,3},{8,4},{9,5... | collective-permute-start | bytes 147464 | tf_op jit(solution)/shard_map/ppermute | solution.py:11
  84.0 22.3 %collective-permute-start.8 = (f32[48,256]{1,0:T(8,128)S(1)}, f32[48,256]{1,0:T(8,128)S(1)}, u32[]{:S(2)}, u32[]{:S(2)}) collective-permute-start(f32[48,256]{1,0:T(8,128)S(1)} %get-tuple-element.76), channel_id=1, source_target_pairs={{0,1},{1,2},{2,3},{3,4},{4,5},{5,6},{6,7},{7,8},{8,9},{9,10},{10,1... | collective-permute-start | bytes 147464 | tf_op jit(solution)/shard_map/ppermute | solution.py:11
  84.1 29.8 %collective-permute-start.9 = (f32[48,256]{1,0:T(8,128)S(1)}, f32[48,256]{1,0:T(8,128)S(1)}, u32[]{:S(2)}, u32[]{:S(2)}) collective-permute-start(f32[48,256]{1,0:T(8,128)S(1)} %get-tuple-element.75), channel_id=1, source_target_pairs={{0,127},{1,0},{2,1},{3,2},{4,3},{5,4},{6,5},{7,6},{8,7},{9,8},{10,... | collective-permute-start | bytes 147464 | tf_op jit(solution)/shard_map/ppermute | solution.py:11
  91.3 22.7 %collective-permute-start.10 = (f32[48,256]{1,0:T(8,128)S(1)}, f32[48,256]{1,0:T(8,128)S(1)}, u32[]{:S(2)}, u32[]{:S(2)}) collective-permute-start(f32[48,256]{1,0:T(8,128)S(1)} %get-tuple-element.74), channel_id=1, source_target_pairs={{0,2},{1,3},{2,4},{3,5},{4,6},{5,7},{6,8},{7,9},{8,10},{9,11},{10,... | collective-permute-start | bytes 147464 | tf_op jit(solution)/shard_map/ppermute | solution.py:11
  91.3 30.9 %collective-permute-start.11 = (f32[48,256]{1,0:T(8,128)S(1)}, f32[48,256]{1,0:T(8,128)S(1)}, u32[]{:S(2)}, u32[]{:S(2)}) collective-permute-start(f32[48,256]{1,0:T(8,128)S(1)} %get-tuple-element.73), channel_id=1, source_target_pairs={{0,126},{1,127},{2,0},{3,1},{4,2},{5,3},{6,4},{7,5},{8,6},{9,7},{1... | collective-permute-start | bytes 147464 | tf_op jit(solution)/shard_map/ppermute | solution.py:11
  98.7 23.5 %collective-permute-start.12 = (f32[48,256]{1,0:T(8,128)S(1)}, f32[48,256]{1,0:T(8,128)S(1)}, u32[]{:S(2)}, u32[]{:S(2)}) collective-permute-start(f32[48,256]{1,0:T(8,128)S(1)} %get-tuple-element.72), channel_id=1, source_target_pairs={{0,3},{1,4},{2,5},{3,6},{4,7},{5,8},{6,9},{7,10},{8,11},{9,12},{10... | collective-permute-start | bytes 147464 | tf_op jit(solution)/shard_map/ppermute | solution.py:11
  106.3 15.9 %collective-permute-start.13 = (f32[48,256]{1,0:T(8,128)S(1)}, f32[48,256]{1,0:T(8,128)S(1)}, u32[]{:S(2)}, u32[]{:S(2)}) collective-permute-start(f32[48,256]{1,0:T(8,128)S(1)} %get-tuple-element.71), channel_id=1, source_target_pairs={{0,125},{1,126},{2,127},{3,0},{4,1},{5,2},{6,3},{7,4},{8,5},{9,6},... | collective-permute-start | bytes 147464 | tf_op jit(solution)/shard_map/ppermute | solution.py:11
  113.9 9.9 %collective-permute-start.14 = (f32[48,256]{1,0:T(8,128)S(1)}, f32[48,256]{1,0:T(8,128)S(1)}, u32[]{:S(2)}, u32[]{:S(2)}) collective-permute-start(f32[48,256]{1,0:T(8,128)S(1)} %get-tuple-element.70), channel_id=1, source_target_pairs={{0,4},{1,5},{2,6},{3,7},{4,8},{5,9},{6,10},{7,11},{8,12},{9,13},{1... | collective-permute-start | bytes 147464 | tf_op jit(solution)/shard_map/ppermute | solution.py:11
  114.0 9.9 %collective-permute-start.15 = (f32[48,256]{1,0:T(8,128)S(1)}, f32[48,256]{1,0:T(8,128)S(1)}, u32[]{:S(2)}, u32[]{:S(2)}) collective-permute-start(f32[48,256]{1,0:T(8,128)S(1)} %get-tuple-element.69), channel_id=1, source_target_pairs={{0,124},{1,125},{2,126},{3,127},{4,0},{5,1},{6,2},{7,3},{8,4},{9,5... | collective-permute-start | bytes 147464 | tf_op jit(solution)/shard_map/ppermute | solution.py:11
  141.3 20.7 %collective-permute-start.16 = (f32[48,256]{1,0:T(8,128)S(1)}, f32[48,256]{1,0:T(8,128)S(1)}, u32[]{:S(2)}, u32[]{:S(2)}) collective-permute-start(f32[48,256]{1,0:T(8,128)S(1)} %get-tuple-element.68), channel_id=1, source_target_pairs={{0,1},{1,2},{2,3},{3,4},{4,5},{5,6},{6,7},{7,8},{8,9},{9,10},{10,1... | collective-permute-start | bytes 147464 | tf_op jit(solution)/shard_map/ppermute | solution.py:11
  141.4 28.1 %collective-permute-start.17 = (f32[48,256]{1,0:T(8,128)S(1)}, f32[48,256]{1,0:T(8,128)S(1)}, u32[]{:S(2)}, u32[]{:S(2)}) collective-permute-start(f32[48,256]{1,0:T(8,128)S(1)} %get-tuple-element.67), channel_id=1, source_target_pairs={{0,127},{1,0},{2,1},{3,2},{4,3},{5,4},{6,5},{7,6},{8,7},{9,8},{10,... | collective-permute-start | bytes 147464 | tf_op jit(solution)/shard_map/ppermute | solution.py:11
  148.6 21.1 %collective-permute-start.18 = (f32[48,256]{1,0:T(8,128)S(1)}, f32[48,256]{1,0:T(8,128)S(1)}, u32[]{:S(2)}, u32[]{:S(2)}) collective-permute-start(f32[48,256]{1,0:T(8,128)S(1)} %get-tuple-element.66), channel_id=1, source_target_pairs={{0,2},{1,3},{2,4},{3,5},{4,6},{5,7},{6,8},{7,9},{8,10},{9,11},{10,... | collective-permute-start | bytes 147464 | tf_op jit(solution)/shard_map/ppermute | solution.py:11
  148.6 29.1 %collective-permute-start.19 = (f32[48,256]{1,0:T(8,128)S(1)}, f32[48,256]{1,0:T(8,128)S(1)}, u32[]{:S(2)}, u32[]{:S(2)}) collective-permute-start(f32[48,256]{1,0:T(8,128)S(1)} %get-tuple-element.65), channel_id=1, source_target_pairs={{0,126},{1,127},{2,0},{3,1},{4,2},{5,3},{6,4},{7,5},{8,6},{9,7},{1... | collective-permute-start | bytes 147464 | tf_op jit(solution)/shard_map/ppermute | solution.py:11
  156.0 21.6 %collective-permute-start.20 = (f32[48,256]{1,0:T(8,128)S(1)}, f32[48,256]{1,0:T(8,128)S(1)}, u32[]{:S(2)}, u32[]{:S(2)}) collective-permute-start(f32[48,256]{1,0:T(8,128)S(1)} %get-tuple-element.64), channel_id=1, source_target_pairs={{0,3},{1,4},{2,5},{3,6},{4,7},{5,8},{6,9},{7,10},{8,11},{9,12},{10... | collective-permute-start | bytes 147464 | tf_op jit(solution)/shard_map/ppermute | solution.py:11
  162.0 15.7 %collective-permute-start.21 = (f32[48,256]{1,0:T(8,128)S(1)}, f32[48,256]{1,0:T(8,128)S(1)}, u32[]{:S(2)}, u32[]{:S(2)}) collective-permute-start(f32[48,256]{1,0:T(8,128)S(1)} %get-tuple-element.63), channel_id=1, source_target_pairs={{0,125},{1,126},{2,127},{3,0},{4,1},{5,2},{6,3},{7,4},{8,5},{9,6},... | collective-permute-start | bytes 147464 | tf_op jit(solution)/shard_map/ppermute | solution.py:11
  169.5 9.9 %collective-permute-start.22 = (f32[48,256]{1,0:T(8,128)S(1)}, f32[48,256]{1,0:T(8,128)S(1)}, u32[]{:S(2)}, u32[]{:S(2)}) collective-permute-start(f32[48,256]{1,0:T(8,128)S(1)} %get-tuple-element.62), channel_id=1, source_target_pairs={{0,4},{1,5},{2,6},{3,7},{4,8},{5,9},{6,10},{7,11},{8,12},{9,13},{1... | collective-permute-start | bytes 147464 | tf_op jit(solution)/shard_map/ppermute | solution.py:11
  169.6 9.8 %collective-permute-start.23 = (f32[48,256]{1,0:T(8,128)S(1)}, f32[48,256]{1,0:T(8,128)S(1)}, u32[]{:S(2)}, u32[]{:S(2)}) collective-permute-start(f32[48,256]{1,0:T(8,128)S(1)} %get-tuple-element.61), channel_id=1, source_target_pairs={{0,124},{1,125},{2,126},{3,127},{4,0},{5,1},{6,2},{7,3},{8,4},{9,5... | collective-permute-start | bytes 147464 | tf_op jit(solution)/shard_map/ppermute | solution.py:11
  196.3 20.4 %collective-permute-start.24 = (f32[48,256]{1,0:T(8,128)S(1)}, f32[48,256]{1,0:T(8,128)S(1)}, u32[]{:S(2)}, u32[]{:S(2)}) collective-permute-start(f32[48,256]{1,0:T(8,128)S(1)} %get-tuple-element.60), channel_id=1, source_target_pairs={{0,1},{1,2},{2,3},{3,4},{4,5},{5,6},{6,7},{7,8},{8,9},{9,10},{10,1... | collective-permute-start | bytes 147464 | tf_op jit(solution)/shard_map/ppermute | solution.py:11
  196.3 27.9 %collective-permute-start.25 = (f32[48,256]{1,0:T(8,128)S(1)}, f32[48,256]{1,0:T(8,128)S(1)}, u32[]{:S(2)}, u32[]{:S(2)}) collective-permute-start(f32[48,256]{1,0:T(8,128)S(1)} %get-tuple-element.59), channel_id=1, source_target_pairs={{0,127},{1,0},{2,1},{3,2},{4,3},{5,4},{6,5},{7,6},{8,7},{9,8},{10,... | collective-permute-start | bytes 147464 | tf_op jit(solution)/shard_map/ppermute | solution.py:11
  203.5 20.8 %collective-permute-start.26 = (f32[48,256]{1,0:T(8,128)S(1)}, f32[48,256]{1,0:T(8,128)S(1)}, u32[]{:S(2)}, u32[]{:S(2)}) collective-permute-start(f32[48,256]{1,0:T(8,128)S(1)} %get-tuple-element.58), channel_id=1, source_target_pairs={{0,2},{1,3},{2,4},{3,5},{4,6},{5,7},{6,8},{7,9},{8,10},{9,11},{10,... | collective-permute-start | bytes 147464 | tf_op jit(solution)/shard_map/ppermute | solution.py:11
  203.5 28.9 %collective-permute-start.27 = (f32[48,256]{1,0:T(8,128)S(1)}, f32[48,256]{1,0:T(8,128)S(1)}, u32[]{:S(2)}, u32[]{:S(2)}) collective-permute-start(f32[48,256]{1,0:T(8,128)S(1)} %get-tuple-element.57), channel_id=1, source_target_pairs={{0,126},{1,127},{2,0},{3,1},{4,2},{5,3},{6,4},{7,5},{8,6},{9,7},{1... | collective-permute-start | bytes 147464 | tf_op jit(solution)/shard_map/ppermute | solution.py:11
  211.0 21.4 %collective-permute-start.28 = (f32[48,256]{1,0:T(8,128)S(1)}, f32[48,256]{1,0:T(8,128)S(1)}, u32[]{:S(2)}, u32[]{:S(2)}) collective-permute-start(f32[48,256]{1,0:T(8,128)S(1)} %get-tuple-element.56), channel_id=1, source_target_pairs={{0,3},{1,4},{2,5},{3,6},{4,7},{5,8},{6,9},{7,10},{8,11},{9,12},{10... | collective-permute-start | bytes 147464 | tf_op jit(solution)/shard_map/ppermute | solution.py:11
  216.7 15.7 %collective-permute-start.29 = (f32[48,256]{1,0:T(8,128)S(1)}, f32[48,256]{1,0:T(8,128)S(1)}, u32[]{:S(2)}, u32[]{:S(2)}) collective-permute-start(f32[48,256]{1,0:T(8,128)S(1)} %get-tuple-element.55), channel_id=1, source_target_pairs={{0,125},{1,126},{2,127},{3,0},{4,1},{5,2},{6,3},{7,4},{8,5},{9,6},... | collective-permute-start | bytes 147464 | tf_op jit(solution)/shard_map/ppermute | solution.py:11
  224.2 9.9 %collective-permute-start.30 = (f32[48,256]{1,0:T(8,128)S(1)}, f32[48,256]{1,0:T(8,128)S(1)}, u32[]{:S(2)}, u32[]{:S(2)}) collective-permute-start(f32[48,256]{1,0:T(8,128)S(1)} %get-tuple-element.54), channel_id=1, source_target_pairs={{0,4},{1,5},{2,6},{3,7},{4,8},{5,9},{6,10},{7,11},{8,12},{9,13},{1... | collective-permute-start | bytes 147464 | tf_op jit(solution)/shard_map/ppermute | solution.py:11
  224.3 9.8 %collective-permute-start.31 = (f32[48,256]{1,0:T(8,128)S(1)}, f32[48,256]{1,0:T(8,128)S(1)}, u32[]{:S(2)}, u32[]{:S(2)}) collective-permute-start(f32[48,256]{1,0:T(8,128)S(1)} %get-tuple-element.53), channel_id=1, source_target_pairs={{0,124},{1,125},{2,126},{3,127},{4,0},{5,1},{6,2},{7,3},{8,4},{9,5... | collective-permute-start | bytes 147464 | tf_op jit(solution)/shard_map/ppermute | solution.py:11
  251.6 20.7 %collective-permute-start.32 = (f32[48,256]{1,0:T(8,128)S(1)}, f32[48,256]{1,0:T(8,128)S(1)}, u32[]{:S(2)}, u32[]{:S(2)}) collective-permute-start(f32[48,256]{1,0:T(8,128)S(1)} %get-tuple-element.52), channel_id=1, source_target_pairs={{0,1},{1,2},{2,3},{3,4},{4,5},{5,6},{6,7},{7,8},{8,9},{9,10},{10,1... | collective-permute-start | bytes 147464 | tf_op jit(solution)/shard_map/ppermute | solution.py:11
  251.6 28.1 %collective-permute-start.33 = (f32[48,256]{1,0:T(8,128)S(1)}, f32[48,256]{1,0:T(8,128)S(1)}, u32[]{:S(2)}, u32[]{:S(2)}) collective-permute-start(f32[48,256]{1,0:T(8,128)S(1)} %get-tuple-element.51), channel_id=1, source_target_pairs={{0,127},{1,0},{2,1},{3,2},{4,3},{5,4},{6,5},{7,6},{8,7},{9,8},{10,... | collective-permute-start | bytes 147464 | tf_op jit(solution)/shard_map/ppermute | solution.py:11
  258.8 21.1 %collective-permute-start.34 = (f32[48,256]{1,0:T(8,128)S(1)}, f32[48,256]{1,0:T(8,128)S(1)}, u32[]{:S(2)}, u32[]{:S(2)}) collective-permute-start(f32[48,256]{1,0:T(8,128)S(1)} %get-tuple-element.50), channel_id=1, source_target_pairs={{0,2},{1,3},{2,4},{3,5},{4,6},{5,7},{6,8},{7,9},{8,10},{9,11},{10,... | collective-permute-start | bytes 147464 | tf_op jit(solution)/shard_map/ppermute | solution.py:11
  258.8 29.1 %collective-permute-start.35 = (f32[48,256]{1,0:T(8,128)S(1)}, f32[48,256]{1,0:T(8,128)S(1)}, u32[]{:S(2)}, u32[]{:S(2)}) collective-permute-start(f32[48,256]{1,0:T(8,128)S(1)} %get-tuple-element.49), channel_id=1, source_target_pairs={{0,126},{1,127},{2,0},{3,1},{4,2},{5,3},{6,4},{7,5},{8,6},{9,7},{1... | collective-permute-start | bytes 147464 | tf_op jit(solution)/shard_map/ppermute | solution.py:11
  266.3 21.7 %collective-permute-start.36 = (f32[48,256]{1,0:T(8,128)S(1)}, f32[48,256]{1,0:T(8,128)S(1)}, u32[]{:S(2)}, u32[]{:S(2)}) collective-permute-start(f32[48,256]{1,0:T(8,128)S(1)} %get-tuple-element.48), channel_id=1, source_target_pairs={{0,3},{1,4},{2,5},{3,6},{4,7},{5,8},{6,9},{7,10},{8,11},{9,12},{10... | collective-permute-start | bytes 147464 | tf_op jit(solution)/shard_map/ppermute | solution.py:11
  272.2 15.7 %collective-permute-start.37 = (f32[48,256]{1,0:T(8,128)S(1)}, f32[48,256]{1,0:T(8,128)S(1)}, u32[]{:S(2)}, u32[]{:S(2)}) collective-permute-start(f32[48,256]{1,0:T(8,128)S(1)} %get-tuple-element.47), channel_id=1, source_target_pairs={{0,125},{1,126},{2,127},{3,0},{4,1},{5,2},{6,3},{7,4},{8,5},{9,6},... | collective-permute-start | bytes 147464 | tf_op jit(solution)/shard_map/ppermute | solution.py:11
  279.8 9.9 %collective-permute-start.38 = (f32[48,256]{1,0:T(8,128)S(1)}, f32[48,256]{1,0:T(8,128)S(1)}, u32[]{:S(2)}, u32[]{:S(2)}) collective-permute-start(f32[48,256]{1,0:T(8,128)S(1)} %get-tuple-element.46), channel_id=1, source_target_pairs={{0,4},{1,5},{2,6},{3,7},{4,8},{5,9},{6,10},{7,11},{8,12},{9,13},{1... | collective-permute-start | bytes 147464 | tf_op jit(solution)/shard_map/ppermute | solution.py:11
  279.9 9.8 %collective-permute-start.39 = (f32[48,256]{1,0:T(8,128)S(1)}, f32[48,256]{1,0:T(8,128)S(1)}, u32[]{:S(2)}, u32[]{:S(2)}) collective-permute-start(f32[48,256]{1,0:T(8,128)S(1)} %get-tuple-element.45), channel_id=1, source_target_pairs={{0,124},{1,125},{2,126},{3,127},{4,0},{5,1},{6,2},{7,3},{8,4},{9,5... | collective-permute-start | bytes 147464 | tf_op jit(solution)/shard_map/ppermute | solution.py:11
  302.5 20.4 %collective-permute-start.40 = (f32[48,256]{1,0:T(8,128)S(1)}, f32[48,256]{1,0:T(8,128)S(1)}, u32[]{:S(2)}, u32[]{:S(2)}) collective-permute-start(f32[48,256]{1,0:T(8,128)S(1)} %get-tuple-element.44), channel_id=1, source_target_pairs={{0,1},{1,2},{2,3},{3,4},{4,5},{5,6},{6,7},{7,8},{8,9},{9,10},{10,1... | collective-permute-start | bytes 147464 | tf_op jit(solution)/shard_map/ppermute | solution.py:11
  302.6 27.8 %collective-permute-start.41 = (f32[48,256]{1,0:T(8,128)S(1)}, f32[48,256]{1,0:T(8,128)S(1)}, u32[]{:S(2)}, u32[]{:S(2)}) collective-permute-start(f32[48,256]{1,0:T(8,128)S(1)} %get-tuple-element.43), channel_id=1, source_target_pairs={{0,127},{1,0},{2,1},{3,2},{4,3},{5,4},{6,5},{7,6},{8,7},{9,8},{10,... | collective-permute-start | bytes 147464 | tf_op jit(solution)/shard_map/ppermute | solution.py:11
  309.8 20.8 %collective-permute-start.42 = (f32[48,256]{1,0:T(8,128)S(1)}, f32[48,256]{1,0:T(8,128)S(1)}, u32[]{:S(2)}, u32[]{:S(2)}) collective-permute-start(f32[48,256]{1,0:T(8,128)S(1)} %get-tuple-element.42), channel_id=1, source_target_pairs={{0,2},{1,3},{2,4},{3,5},{4,6},{5,7},{6,8},{7,9},{8,10},{9,11},{10,... | collective-permute-start | bytes 147464 | tf_op jit(solution)/shard_map/ppermute | solution.py:11
  309.8 28.6 %collective-permute-start.43 = (f32[48,256]{1,0:T(8,128)S(1)}, f32[48,256]{1,0:T(8,128)S(1)}, u32[]{:S(2)}, u32[]{:S(2)}) collective-permute-start(f32[48,256]{1,0:T(8,128)S(1)} %get-tuple-element.41), channel_id=1, source_target_pairs={{0,126},{1,127},{2,0},{3,1},{4,2},{5,3},{6,4},{7,5},{8,6},{9,7},{1... | collective-permute-start | bytes 147464 | tf_op jit(solution)/shard_map/ppermute | solution.py:11
  317.2 21.1 %collective-permute-start.44 = (f32[48,256]{1,0:T(8,128)S(1)}, f32[48,256]{1,0:T(8,128)S(1)}, u32[]{:S(2)}, u32[]{:S(2)}) collective-permute-start(f32[48,256]{1,0:T(8,128)S(1)} %get-tuple-element.40), channel_id=1, source_target_pairs={{0,3},{1,4},{2,5},{3,6},{4,7},{5,8},{6,9},{7,10},{8,11},{9,12},{10... | collective-permute-start | bytes 147464 | tf_op jit(solution)/shard_map/ppermute | solution.py:11
  322.9 15.5 %collective-permute-start.45 = (f32[48,256]{1,0:T(8,128)S(1)}, f32[48,256]{1,0:T(8,128)S(1)}, u32[]{:S(2)}, u32[]{:S(2)}) collective-permute-start(f32[48,256]{1,0:T(8,128)S(1)} %get-tuple-element.39), channel_id=1, source_target_pairs={{0,125},{1,126},{2,127},{3,0},{4,1},{5,2},{6,3},{7,4},{8,5},{9,6},... | collective-permute-start | bytes 147464 | tf_op jit(solution)/shard_map/ppermute | solution.py:11
  330.5 9.9 %collective-permute-start.46 = (f32[48,256]{1,0:T(8,128)S(1)}, f32[48,256]{1,0:T(8,128)S(1)}, u32[]{:S(2)}, u32[]{:S(2)}) collective-permute-start(f32[48,256]{1,0:T(8,128)S(1)} %get-tuple-element.38), channel_id=1, source_target_pairs={{0,4},{1,5},{2,6},{3,7},{4,8},{5,9},{6,10},{7,11},{8,12},{9,13},{1... | collective-permute-start | bytes 147464 | tf_op jit(solution)/shard_map/ppermute | solution.py:11
  330.6 9.8 %collective-permute-start.47 = (f32[48,256]{1,0:T(8,128)S(1)}, f32[48,256]{1,0:T(8,128)S(1)}, u32[]{:S(2)}, u32[]{:S(2)}) collective-permute-start(f32[48,256]{1,0:T(8,128)S(1)} %get-tuple-element.37), channel_id=1, source_target_pairs={{0,124},{1,125},{2,126},{3,127},{4,0},{5,1},{6,2},{7,3},{8,4},{9,5... | collective-permute-start | bytes 147464 | tf_op jit(solution)/shard_map/ppermute | solution.py:11
  (95 other events, 928.6 us)
where the time goes:
time: 346 us; the launch traced here: 342 us
  starting transfers between devices  183 us (53%)
  local copies, waits for them, and re-layouts  83.4 us (24%)
  matrix products  56.9 us (16%)
  waiting for transfers between devices  8.79 us (3%)
  other arithmetic  7.96 us (2%)
    ppermute x48, starting transfers between devices, from_behind(): lax.ppermute(x, axis, [(i, (i + by) % devices) for i in range(devices)])  183 us
    gather x48, local copies, waits for them, and re-layouts, apply(): picked = own_blocks[jnp.minimum(column, block_count - 1)]  66.7 us
    dot_general x48, matrix products, apply(): jnp.einsum('rij,rjp->rip', weights, picked, precision=lax.Precision.HIGHEST)  43.8 us
    gather x6, local copies, waits for them, and re-layouts, gather_halo(): payloads = state[send_rows]  11.1 us
    ppermute x48, waiting for transfers between devices, from_behind(): lax.ppermute(x, axis, [(i, (i + by) % devices) for i in range(devices)])  8.79 us
  transfers between devices with their start and end apart: 48, of which 6 were waited for; matrix products, arithmetic and copies ran while one was open for 18% of the time, Pallas kernels for 0%

commit v1 on v0

v1 whole, which is shorter than its diff:
```python
import functools

import jax
import jax.numpy as jnp
from jax import lax
from jax.experimental import pallas as pl
from jax.experimental.pallas import tpu as pltpu
from jax.sharding import PartitionSpec as P

STEPS = 3
LANES = 128
MESH = pl.DeviceIdType.MESH
F32 = jnp.float32
BF16 = jnp.bfloat16


def partner_offset(offset_index):
    return (offset_index // 2 + 1) * (1 if offset_index % 2 == 0 else -1)


def split2(x):
    hi = x.astype(BF16)
    lo = (x - hi.astype(F32)).astype(BF16)
    return hi, lo


def dot(a, b):
    return jnp.dot(a, b, preferred_element_type=F32)


def product(w_hi, w_lo, cat):
    wide = dot(w_hi, cat)
    return (wide[:, :LANES] + wide[:, LANES:]) + dot(w_lo, cat[:, :LANES])


def kernel(
    devices,
    v0_hbm,
    src_hbm,
    et_hbm,
    it_hbm,
    ec_hbm,
    ic_hbm,
    send_hbm,
    out_ref,
    v0,
    src,
    tiles,
    cols,
    send_v,
    square,
    pick,
    w_hi,
    w_lo,
    pay,
    halo,
    vcat,
    vpart,
    part,
    psrc,
    load_sem,
    send_sem,
    recv_sem,
):
    partners, per_list = send_v.shape
    own = v0.shape[0]
    listed = partners * per_list
    blocks, slots, size, _ = et_hbm.shape
    ext_blocks = (own + listed) // size
    halves = v0.shape[1] // LANES
    exchanges = 2 * STEPS

    me = lax.axis_index("rows")
    targets = [lax.rem(me + partner_offset(o) + devices, devices) for o in range(partners)]

    barrier = pltpu.get_barrier_semaphore()
    for target in targets:
        pl.semaphore_signal(barrier, inc=1, device_id=(target,), device_id_type=MESH)

    loads = [
        pltpu.make_async_copy(send_hbm, send_v, load_sem.at[0]),
        pltpu.make_async_copy(v0_hbm, v0, load_sem.at[1]),
        pltpu.make_async_copy(et_hbm, tiles.at[0], load_sem.at[2]),
        pltpu.make_async_copy(ec_hbm, cols.at[0], load_sem.at[3]),
        pltpu.make_async_copy(src_hbm, src, load_sem.at[4]),
        pltpu.make_async_copy(it_hbm, tiles.at[1], load_sem.at[5]),
        pltpu.make_async_copy(ic_hbm, cols.at[1], load_sem.at[6]),
    ]
    for load in loads:
        load.start()

    def copies(exchange, half):
        order = sorted(range(partners), key=lambda o: -abs(partner_offset(o)))
        return [
            pltpu.make_async_remote_copy(
                src_ref=pay.at[exchange, half, pl.ds(o * per_list, per_list)],
                dst_ref=halo.at[exchange, half, pl.ds(o * per_list, per_list)],
                send_sem=send_sem.at[exchange, half, o],
                recv_sem=recv_sem.at[exchange, half, o],
                device_id=(targets[o],),
                device_id_type=MESH,
            )
            for o in order
        ]

    square[...] = jnp.zeros_like(square)
    loads[0].wait()
    square[0:partners, 0:per_list] = send_v[...].astype(F32)
    turned = square[...].T
    lane = lax.broadcasted_iota(jnp.int32, (per_list, LANES), 1).astype(F32)
    for o in range(partners):
        column = jnp.broadcast_to(turned[0:per_list, o : o + 1], (per_list, LANES))
        for c in range(own // LANES):
            pick[o * per_list : (o + 1) * per_list, c * LANES : (c + 1) * LANES] = jnp.where(
                column == lane + float(c * LANES), 1.0, 0.0
            ).astype(BF16)

    def picked(x):
        hi, mid = split2(x)
        low = ((x - hi.astype(F32)) - mid.astype(F32)).astype(BF16)
        wide = dot(pick[...], jnp.concatenate([hi, mid], axis=1))
        return (wide[:, :LANES] + wide[:, LANES:]) + dot(pick[...], low)

    loads[1].wait()
    for half in range(halves):
        pay[0, half] = picked(v0[:, half * LANES : (half + 1) * LANES])
        if half == 0:
            pl.semaphore_wait(barrier, partners)
        for copy in copies(0, half):
            copy.start()

    def build(which):
        for g in range(blocks):
            named = [cols[which, g, k] for k in range(slots)]
            for c in range(ext_blocks):
                total = None
                for k in range(slots):
                    term = tiles[which, g, k] * jnp.where(named[k] == c, 1.0, 0.0).astype(F32)
                    total = term if total is None else total + term
                hi, lo = split2(total)
                rows = slice(listed + g * size, listed + (g + 1) * size)
                w_hi[which, rows, c * size : (c + 1) * size] = hi
                w_lo[which, rows, c * size : (c + 1) * size] = lo
        for w in (w_hi, w_lo):
            w[which, 0:listed] = dot(pick[...], w[which, listed:]).astype(BF16)

    loads[2].wait()
    loads[3].wait()
    build(0)
    loads[4].wait()
    for half in range(halves):
        psrc[half] = picked(src[:, half * LANES : (half + 1) * LANES])

    def own_part(which, half, state, payload, with_source):
        hi, lo = split2(state)
        vcat[half, :, 0:LANES] = hi
        vcat[half, :, LANES:] = lo
        near = product(w_hi[which, :, 0:own], w_lo[which, :, 0:own], vcat[half])
        head, body = payload + near[0:listed], state + near[listed:]
        if with_source:
            head = head + psrc[half]
            body = body + src[:, half * LANES : (half + 1) * LANES]
        part[half] = head
        vpart[half] = body

    for half in range(halves):
        own_part(0, half, v0[:, half * LANES : (half + 1) * LANES], pay[0, half], True)
    loads[5].wait()
    loads[6].wait()
    build(1)

    def stage(exchange, which, half, last):
        for copy in copies(exchange, half):
            copy.wait_recv()
        hi, lo = split2(halo[exchange, half])
        hcat = jnp.concatenate([hi, lo], axis=1)
        if not last:
            payload = part[half] + product(
                w_hi[which, 0:listed, own:], w_lo[which, 0:listed, own:], hcat
            )
            pay[exchange + 1, half] = payload
            for copy in copies(exchange + 1, half):
                copy.start()
        state = vpart[half] + product(
            w_hi[which, listed:, own:], w_lo[which, listed:, own:], hcat
        )
        if last:
            out_ref[:, half * LANES : (half + 1) * LANES] = state
        else:
            own_part(1 - which, half, state, pay[exchange + 1, half], which == 1)

    for exchange in range(exchanges):
        for half in range(halves):
            stage(exchange, exchange % 2, half, exchange == exchanges - 1)

    for exchange in range(exchanges):
        for half in range(halves):
            for copy in copies(exchange, half):
                copy.wait_send()


def on_device(devices, v0, source, et, it, ec, ic, send):
    own, panels = v0.shape
    partners, per_list = send.shape
    blocks, slots, size, _ = et.shape
    listed = partners * per_list
    extended = own + listed
    halves = panels // LANES
    exchanges = 2 * STEPS
    any_spec = pl.BlockSpec(memory_space=pl.ANY)
    return pl.pallas_call(
        functools.partial(kernel, devices),
        out_shape=jax.ShapeDtypeStruct((own, panels), F32),
        in_specs=[any_spec] * 7,
        out_specs=pl.BlockSpec(memory_space=pltpu.VMEM),
        scratch_shapes=[
            pltpu.VMEM((own, panels), F32),
            pltpu.VMEM((own, panels), F32),
            pltpu.VMEM((2, blocks, slots, size, size), F32),
            pltpu.SMEM((2, blocks, slots), jnp.int32),
            pltpu.VMEM((partners, per_list), jnp.int32),
            pltpu.VMEM((LANES, LANES), F32),
            pltpu.VMEM((listed, own), BF16),
            pltpu.VMEM((2, extended, extended), BF16),
            pltpu.VMEM((2, extended, extended), BF16),
            pltpu.VMEM((exchanges, halves, listed, LANES), F32),
            pltpu.VMEM((exchanges, halves, listed, LANES), F32),
            pltpu.VMEM((halves, own, 2 * LANES), BF16),
            pltpu.VMEM((halves, own, LANES), F32),
            pltpu.VMEM((halves, listed, LANES), F32),
            pltpu.VMEM((halves, listed, LANES), F32),
            pltpu.SemaphoreType.DMA((7,)),
            pltpu.SemaphoreType.DMA((exchanges, halves, partners)),
            pltpu.SemaphoreType.DMA((exchanges, halves, partners)),
        ],
        compiler_params=pltpu.CompilerParams(
            collective_id=0, has_side_effects=True, vmem_limit_bytes=48 * 1024 * 1024
        ),
    )(v0, source, et, it, ec, ic, send)


def solution(mesh):
    return jax.shard_map(
        functools.partial(on_device, mesh.shape["rows"]),
        mesh=mesh,
        in_specs=(
            P("rows", None),
            P("rows", None),
            P("rows", None, None, None),
            P("rows", None, None, None),
            P("rows", None),
            P("rows", None),
            P("rows", None),
        ),
        out_specs=P("rows", None),
        check_vma=False,
    )
```

time: 346 us -> 67.3 us (0.19)
  the two profiles are of different devices: /device:TPU:0 before, /device:TPU:1 now
where the time goes in v1:
time: 67.3 us; the launch traced here: 66.9 us
  Pallas kernels  58.8 us (87%)
  local copies, waits for them, and re-layouts  8.11 us (12%)
    pallas_call x1, Pallas kernels, on_device(): pl.pallas_call(functools.partial(kernel, devices), out_shape=jax.ShapeDty...  58.8 us
    unnamed x15, local copies, waits for them, and re-layouts  8.11 us

profile of v1, /device:TPU:1, one launch (start us, length us, event | category | flops | bytes accessed | tf_op | source)
XLA Modules:
  0.0 66.9 jit_solution(7948893376816658558)
XLA Ops:
  0.0 0.0 copy-start
  0.0 1.6 %copy-done = f32[4,8,128,128]{3,2,1,0:T(8,128)S(1)} copy-done((f32[4,8,128,128]{3,2,1,0:T(8,128)S(1)}, f32[4,8,128,128]{3,2,1,0:T(8,128)}, u32[]{:S(2)}) %copy-start) | copy-done | bytes 2097176
  1.6 0.0 copy-start.1
  1.6 1.6 %copy-done.1 = f32[4,8,128,128]{3,2,1,0:T(8,128)S(1)} copy-done((f32[4,8,128,128]{3,2,1,0:T(8,128)S(1)}, f32[4,8,128,128]{3,2,1,0:T(8,128)}, u32[]{:S(2)}) %copy-start.1) | copy-done | bytes 2097176
  3.2 0.0 copy-start.2
  3.2 1.0 %copy-done.2 = f32[512,256]{1,0:T(8,128)S(1)} copy-done((f32[512,256]{1,0:T(8,128)S(1)}, f32[512,256]{1,0:T(8,128)}, u32[]{:S(2)}) %copy-start.2) | copy-done | bytes 524312
  4.2 0.0 copy-start.3
  4.2 1.0 %copy-done.3 = f32[512,256]{1,0:T(8,128)S(1)} copy-done((f32[512,256]{1,0:T(8,128)S(1)}, f32[512,256]{1,0:T(8,128)}, u32[]{:S(2)}) %copy-start.3) | copy-done | bytes 524312
  5.3 0.0 copy-start.4
  5.3 0.7 %copy-done.4 = s32[8,48]{1,0:T(8,128)S(1)} copy-done((s32[8,48]{1,0:T(8,128)S(1)}, s32[8,48]{1,0:T(8,128)}, u32[]{:S(2)}) %copy-start.4) | copy-done | bytes 1560
  6.0 0.0 copy-start.5
  6.0 0.7 %copy-done.5 = s32[4,8]{1,0:T(4,128)S(1)} copy-done((s32[4,8]{1,0:T(4,128)S(1)}, s32[4,8]{1,0:T(4,128)}, u32[]{:S(2)}) %copy-start.5) | copy-done | bytes 152
  6.6 0.0 copy-start.6
  6.6 0.7 %copy-done.6 = s32[4,8]{1,0:T(4,128)S(1)} copy-done((s32[4,8]{1,0:T(4,128)S(1)}, s32[4,8]{1,0:T(4,128)}, u32[]{:S(2)}) %copy-start.6) | copy-done | bytes 152
  7.3 58.8 %shard_map.73 = f32[512,256]{1,0:T(8,128)S(1)} custom-call(f32[512,256]{1,0:T(8,128)S(1)} %copy-done.2, f32[512,256]{1,0:T(8,128)S(1)} %copy-done.3, f32[4,8,128,128]{3,2,1,0:T(8,128)S(1)} %copy-done, f32[4,8,128,128]{3,2,1,0:T(8,128)S(1)} %copy-done.1, s32[4,8]{1,0:T(4,128)S(1)} %copy-done.5, s32[4,8]{1,0:T(4,128)S(1)} %copy-done.6, s32[8,48]{1,0:T(8,128)S(1)} %copy-done.4), custom_call_target="tpu_custom_call" | custom-call | tf_op jit(solution)/shard_map/pallas_call | solution.py:211
  66.1 0.8 %copy.9 = f32[512,256]{1,0:T(8,128)} copy(f32[512,256]{1,0:T(8,128)S(1)} %shard_map.73) | data formatting | bytes 1048576
Async XLA Ops:
  0.0 1.6 %copy-start = (f32[4,8,128,128]{3,2,1,0:T(8,128)S(1)}, f32[4,8,128,128]{3,2,1,0:T(8,128)}, u32[]{:S(2)}) copy-start(f32[4,8,128,128]{3,2,1,0:T(8,128)} %et_hbm.1) | copy-start | bytes 6291460
  1.6 1.6 %copy-start.1 = (f32[4,8,128,128]{3,2,1,0:T(8,128)S(1)}, f32[4,8,128,128]{3,2,1,0:T(8,128)}, u32[]{:S(2)}) copy-start(f32[4,8,128,128]{3,2,1,0:T(8,128)} %it_hbm.1) | copy-start | bytes 6291460
  3.2 1.0 %copy-start.2 = (f32[512,256]{1,0:T(8,128)S(1)}, f32[512,256]{1,0:T(8,128)}, u32[]{:S(2)}) copy-start(f32[512,256]{1,0:T(8,128)} %v0_hbm.1) | copy-start | bytes 1572868
  4.2 1.0 %copy-start.3 = (f32[512,256]{1,0:T(8,128)S(1)}, f32[512,256]{1,0:T(8,128)}, u32[]{:S(2)}) copy-start(f32[512,256]{1,0:T(8,128)} %src_hbm.1) | copy-start | bytes 1572868
  5.3 0.7 %copy-start.4 = (s32[8,48]{1,0:T(8,128)S(1)}, s32[8,48]{1,0:T(8,128)}, u32[]{:S(2)}) copy-start(s32[8,48]{1,0:T(8,128)} %send_hbm.1) | copy-start | bytes 4612
  6.0 0.7 %copy-start.5 = (s32[4,8]{1,0:T(4,128)S(1)}, s32[4,8]{1,0:T(4,128)}, u32[]{:S(2)}) copy-start(s32[4,8]{1,0:T(4,128)} %ec_hbm.1) | copy-start | bytes 388
  6.6 0.7 %copy-start.6 = (s32[4,8]{1,0:T(4,128)S(1)}, s32[4,8]{1,0:T(4,128)}, u32[]{:S(2)}) copy-start(s32[4,8]{1,0:T(4,128)} %ic_hbm.1) | copy-start | bytes 388

commit v2 on v1

--- a/solution.py
+++ b/solution.py
@@ -207,11 +207,11 @@
     extended = own + listed
     halves = panels // LANES
     exchanges = 2 * STEPS
-    any_spec = pl.BlockSpec(memory_space=pl.ANY)
+    in_hbm = pl.BlockSpec(memory_space=pltpu.HBM)
     return pl.pallas_call(
         functools.partial(kernel, devices),
         out_shape=jax.ShapeDtypeStruct((own, panels), F32),
-        in_specs=[any_spec] * 7,
+        in_specs=[in_hbm] * 7,
         out_specs=pl.BlockSpec(memory_space=pltpu.VMEM),
         scratch_shapes=[
             pltpu.VMEM((own, panels), F32),
@@ -236,7 +236,12 @@
         compiler_params=pltpu.CompilerParams(
             collective_id=0, has_side_effects=True, vmem_limit_bytes=48 * 1024 * 1024
         ),
-    )(v0, source, et, it, ec, ic, send)
+    )(
+        *[
+            pltpu.with_memory_space_constraint(x, pltpu.HBM)
+            for x in (v0, source, et, it, ec, ic, send)
+        ]
+    )
 
 
 def solution(mesh):

time: 67.3 us -> 59.7 us (0.89)
  local copies, waits for them, and re-layouts: 8.11 us -> 0.8 us
    unnamed x15 -> x1, local copies, waits for them, and re-layouts: 8.11 us -> 0.8 us
where the time goes in v2:
time: 59.7 us; the launch traced here: 59.6 us
  Pallas kernels  58.8 us (98%)
  local copies, waits for them, and re-layouts  0.8 us (1%)
    pallas_call x1, Pallas kernels, on_device(): pl.pallas_call(functools.partial(kernel, devices), out_shape=jax.ShapeDty...  58.8 us

profile of v2, /device:TPU:1, one launch (start us, length us, event | category | flops | bytes accessed | tf_op | source)
XLA Modules:
  0.0 59.6 jit_solution(16656109800744429323)
XLA Ops:
  0.0 58.8 %shard_map.73 = f32[512,256]{1,0:T(8,128)S(1)} custom-call(f32[512,256]{1,0:T(8,128)} %v0_hbm.1, f32[512,256]{1,0:T(8,128)} %src_hbm.1, f32[4,8,128,128]{3,2,1,0:T(8,128)} %et_hbm.1, f32[4,8,128,128]{3,2,1,0:T(8,128)} %it_hbm.1, s32[4,8]{1,0:T(4,128)} %ec_hbm.1, s32[4,8]{1,0:T(4,128)} %ic_hbm.1, s32[8,48]{1,0:T(8,128)} %send_hbm.1), custom_call_target="tpu_custom_call" | custom-call | tf_op jit(solution)/shard_map/pallas_call | solution.py:211
  58.8 0.8 %copy.9 = f32[512,256]{1,0:T(8,128)} copy(f32[512,256]{1,0:T(8,128)S(1)} %shard_map.73) | data formatting | bytes 1048576

commit v3 on v2

--- a/solution.py
+++ b/solution.py
@@ -90,7 +90,6 @@
         load.start()
 
     def copies(exchange, half):
-        order = sorted(range(partners), key=lambda o: -abs(partner_offset(o)))
         return [
             pltpu.make_async_remote_copy(
                 src_ref=pay.at[exchange, half, pl.ds(o * per_list, per_list)],
@@ -100,8 +99,19 @@
                 device_id=(targets[o],),
                 device_id_type=MESH,
             )
-            for o in order
+            for o in range(partners)
         ]
+
+    def send(exchange, half):
+        ready = copies(exchange, half)
+        near = sorted(range(partners), key=lambda o: abs(partner_offset(o)))
+        for core in range(2):
+            order = sorted(near, key=lambda o: (partner_offset(o) + core) % 2)
+
+            @pl.when(lax.rem(me, 2) == core)
+            def _():
+                for o in order:
+                    ready[o].start()
 
     square[...] = jnp.zeros_like(square)
     loads[0].wait()
@@ -126,8 +136,7 @@
         pay[0, half] = picked(v0[:, half * LANES : (half + 1) * LANES])
         if half == 0:
             pl.semaphore_wait(barrier, partners)
-        for copy in copies(0, half):
-            copy.start()
+        send(0, half)
 
     def build(which):
         for g in range(blocks):
@@ -179,8 +188,7 @@
                 w_hi[which, 0:listed, own:], w_lo[which, 0:listed, own:], hcat
             )
             pay[exchange + 1, half] = payload
-            for copy in copies(exchange + 1, half):
-                copy.start()
+            send(exchange + 1, half)
         state = vpart[half] + product(
             w_hi[which, listed:, own:], w_lo[which, listed:, own:], hcat
         )

time: 59.7 us -> 55.9 us (0.936)
  Pallas kernels: 58.8 us -> 55 us
    pallas_call x1, Pallas kernels: 58.8 us -> 55 us  [on_device(): pl.pallas_call(functools.partial(kernel, devices), out_shape=jax.ShapeDty...]
where the time goes in v3:
time: 55.9 us; the launch traced here: 55.8 us
  Pallas kernels  55 us (98%)
  local copies, waits for them, and re-layouts  0.8 us (1%)
    pallas_call x1, Pallas kernels, on_device(): pl.pallas_call(functools.partial(kernel, devices), out_shape=jax.ShapeDty...  55 us

profile of v3, /device:TPU:1, one launch (start us, length us, event | category | flops | bytes accessed | tf_op | source)
XLA Modules:
  0.0 55.8 jit_solution(11643963148501619124)
XLA Ops:
  0.0 55.0 %shard_map.73 = f32[512,256]{1,0:T(8,128)S(1)} custom-call(f32[512,256]{1,0:T(8,128)} %v0_hbm.1, f32[512,256]{1,0:T(8,128)} %src_hbm.1, f32[4,8,128,128]{3,2,1,0:T(8,128)} %et_hbm.1, f32[4,8,128,128]{3,2,1,0:T(8,128)} %it_hbm.1, s32[4,8]{1,0:T(4,128)} %ec_hbm.1, s32[4,8]{1,0:T(4,128)} %ic_hbm.1, s32[8,48]{1,0:T(8,128)} %send_hbm.1), custom_call_target="tpu_custom_call" | custom-call | tf_op jit(solution)/shard_map/pallas_call | solution.py:219
  55.0 0.8 %copy.9 = f32[512,256]{1,0:T(8,128)} copy(f32[512,256]{1,0:T(8,128)S(1)} %shard_map.73) | data formatting | bytes 1048576

commit v4 on v3

--- a/solution.py
+++ b/solution.py
@@ -55,6 +55,7 @@
     pay,
     halo,
     vcat,
+    hcat,
     vpart,
     part,
     psrc,
@@ -69,6 +70,8 @@
     ext_blocks = (own + listed) // size
     halves = v0.shape[1] // LANES
     exchanges = 2 * STEPS
+    packed = listed // 2
+    run = per_list // 2
 
     me = lax.axis_index("rows")
     targets = [lax.rem(me + partner_offset(o) + devices, devices) for o in range(partners)]
@@ -89,21 +92,21 @@
     for load in loads:
         load.start()
 
-    def copies(exchange, half):
+    def copies(exchange, group):
         return [
             pltpu.make_async_remote_copy(
-                src_ref=pay.at[exchange, half, pl.ds(o * per_list, per_list)],
-                dst_ref=halo.at[exchange, half, pl.ds(o * per_list, per_list)],
-                send_sem=send_sem.at[exchange, half, o],
-                recv_sem=recv_sem.at[exchange, half, o],
+                src_ref=pay.at[exchange, group, pl.ds(o * run, run)],
+                dst_ref=halo.at[exchange, group, pl.ds(o * run, run)],
+                send_sem=send_sem.at[exchange, group, o],
+                recv_sem=recv_sem.at[exchange, group, o],
                 device_id=(targets[o],),
                 device_id_type=MESH,
             )
             for o in range(partners)
         ]
 
-    def send(exchange, half):
-        ready = copies(exchange, half)
+    def send(exchange, group):
+        ready = copies(exchange, group)
         near = sorted(range(partners), key=lambda o: abs(partner_offset(o)))
         for core in range(2):
             order = sorted(near, key=lambda o: (partner_offset(o) + core) % 2)
@@ -117,13 +120,35 @@
     loads[0].wait()
     square[0:partners, 0:per_list] = send_v[...].astype(F32)
     turned = square[...].T
-    lane = lax.broadcasted_iota(jnp.int32, (per_list, LANES), 1).astype(F32)
-    for o in range(partners):
-        column = jnp.broadcast_to(turned[0:per_list, o : o + 1], (per_list, LANES))
-        for c in range(own // LANES):
-            pick[o * per_list : (o + 1) * per_list, c * LANES : (c + 1) * LANES] = jnp.where(
-                column == lane + float(c * LANES), 1.0, 0.0
-            ).astype(BF16)
+    column = jnp.concatenate(
+        [
+            jnp.broadcast_to(turned[part_at * run : (part_at + 1) * run, o : o + 1], (run, LANES))
+            for part_at in range(2)
+            for o in range(partners)
+        ],
+        axis=0,
+    )
+    lane = lax.broadcasted_iota(jnp.int32, (listed, LANES), 1).astype(F32)
+    for c in range(own // LANES):
+        pick[:, c * LANES : (c + 1) * LANES] = jnp.where(
+            column == lane + float(c * LANES), 1.0, 0.0
+        ).astype(BF16)
+
+    first = lax.broadcasted_iota(jnp.int32, (packed, LANES), 1) < LANES // 2
+
+    def turn(x):
+        return pltpu.roll(x, LANES // 2, 1)
+
+    def pack(rows):
+        one, two = rows[0:packed], rows[packed:]
+        return jnp.where(first, one, turn(two)), jnp.where(first, turn(one), two)
+
+    def unpack(x):
+        turned_x = turn(x)
+        lists = (partners, run, LANES)
+        left = [jnp.where(first, y, 0.0).reshape(lists) for y in (x, turned_x)]
+        right = [jnp.where(first, 0.0, y).reshape(lists) for y in (turned_x, x)]
+        return [jnp.concatenate(y, axis=1).reshape(listed, LANES) for y in (left, right)]
 
     def picked(x):
         hi, mid = split2(x)
@@ -133,10 +158,12 @@
 
     loads[1].wait()
     for half in range(halves):
-        pay[0, half] = picked(v0[:, half * LANES : (half + 1) * LANES])
-        if half == 0:
-            pl.semaphore_wait(barrier, partners)
-        send(0, half)
+        groups = pack(picked(v0[:, half * LANES : (half + 1) * LANES]))
+        for q in range(2):
+            pay[0, 2 * half + q] = groups[q]
+            if half == 0 and q == 0:
+                pl.semaphore_wait(barrier, partners)
+            send(0, 2 * half + q)
 
     def build(which):
         for g in range(blocks):
@@ -160,50 +187,63 @@
     for half in range(halves):
         psrc[half] = picked(src[:, half * LANES : (half + 1) * LANES])
 
-    def own_part(which, half, state, payload, with_source):
+    def own_part(which, half, state, exchange, with_source):
         hi, lo = split2(state)
         vcat[half, :, 0:LANES] = hi
         vcat[half, :, LANES:] = lo
         near = product(w_hi[which, :, 0:own], w_lo[which, :, 0:own], vcat[half])
-        head, body = payload + near[0:listed], state + near[listed:]
+        head, body = near[0:listed], state + near[listed:]
         if with_source:
             head = head + psrc[half]
             body = body + src[:, half * LANES : (half + 1) * LANES]
-        part[half] = head
+        groups = pack(head)
+        for q in range(2):
+            part[2 * half + q] = pay[exchange, 2 * half + q] + groups[q]
         vpart[half] = body
 
     for half in range(halves):
-        own_part(0, half, v0[:, half * LANES : (half + 1) * LANES], pay[0, half], True)
+        own_part(0, half, v0[:, half * LANES : (half + 1) * LANES], 0, True)
     loads[5].wait()
     loads[6].wait()
     build(1)
 
     def stage(exchange, which, half, last):
-        for copy in copies(exchange, half):
-            copy.wait_recv()
-        hi, lo = split2(halo[exchange, half])
-        hcat = jnp.concatenate([hi, lo], axis=1)
-        if not last:
-            payload = part[half] + product(
-                w_hi[which, 0:listed, own:], w_lo[which, 0:listed, own:], hcat
-            )
-            pay[exchange + 1, half] = payload
-            send(exchange + 1, half)
+        for q in range(2):
+            group = 2 * half + q
+            for copy in copies(exchange, group):
+                copy.wait_recv()
+            left, right = [
+                jnp.concatenate(split2(x), axis=1) for x in unpack(halo[exchange, group])
+            ]
+            if not last:
+                payload = part[group]
+                wide = dot(w_hi[which, 0:packed, own:], left)
+                wide = wide + dot(w_hi[which, packed:listed, own:], right)
+                low = dot(w_lo[which, 0:packed, own:], left[:, :LANES])
+                low = low + dot(w_lo[which, packed:listed, own:], right[:, :LANES])
+                pay[exchange + 1, group] = payload + (
+                    (wide[:, :LANES] + wide[:, LANES:]) + low
+                )
+                send(exchange + 1, group)
+            if q == 0:
+                hcat[...] = left
+            else:
+                hcat[...] = hcat[...] + right
         state = vpart[half] + product(
-            w_hi[which, listed:, own:], w_lo[which, listed:, own:], hcat
+            w_hi[which, listed:, own:], w_lo[which, listed:, own:], hcat[...]
         )
         if last:
             out_ref[:, half * LANES : (half + 1) * LANES] = state
         else:
-            own_part(1 - which, half, state, pay[exchange + 1, half], which == 1)
+            own_part(1 - which, half, state, exchange + 1, which == 1)
 
     for exchange in range(exchanges):
         for half in range(halves):
             stage(exchange, exchange % 2, half, exchange == exchanges - 1)
 
     for exchange in range(exchanges):
-        for half in range(halves):
-            for copy in copies(exchange, half):
+        for group in range(2 * halves):
+            for copy in copies(exchange, group):
                 copy.wait_send()
 
 
@@ -231,15 +271,16 @@
             pltpu.VMEM((listed, own), BF16),
             pltpu.VMEM((2, extended, extended), BF16),
             pltpu.VMEM((2, extended, extended), BF16),
-            pltpu.VMEM((exchanges, halves, listed, LANES), F32),
-            pltpu.VMEM((exchanges, halves, listed, LANES), F32),
+            pltpu.VMEM((exchanges, 2 * halves, listed // 2, LANES), F32),
+            pltpu.VMEM((exchanges, 2 * halves, listed // 2, LANES), F32),
             pltpu.VMEM((halves, own, 2 * LANES), BF16),
+            pltpu.VMEM((listed, 2 * LANES), BF16),
             pltpu.VMEM((halves, own, LANES), F32),
-            pltpu.VMEM((halves, listed, LANES), F32),
+            pltpu.VMEM((2 * halves, listed // 2, LANES), F32),
             pltpu.VMEM((halves, listed, LANES), F32),
             pltpu.SemaphoreType.DMA((7,)),
-            pltpu.SemaphoreType.DMA((exchanges, halves, partners)),
-            pltpu.SemaphoreType.DMA((exchanges, halves, partners)),
+            pltpu.SemaphoreType.DMA((exchanges, 2 * halves, partners)),
+            pltpu.SemaphoreType.DMA((exchanges, 2 * halves, partners)),
         ],
         compiler_params=pltpu.CompilerParams(
             collective_id=0, has_side_effects=True, vmem_limit_bytes=48 * 1024 * 1024

time: 55.9 us -> 55.8 us (level)
  no operation moved by 1% of the time
where the time goes in v4:
time: 55.8 us; the launch traced here: 55.7 us
  Pallas kernels  54.9 us (98%)
  local copies, waits for them, and re-layouts  0.8 us (1%)
    pallas_call x1, Pallas kernels, on_device(): pl.pallas_call(functools.partial(kernel, devices), out_shape=jax.ShapeDty...  54.9 us

profile of v4, /device:TPU:1, one launch (start us, length us, event | category | flops | bytes accessed | tf_op | source)
XLA Modules:
  0.0 55.7 jit_solution(13507771810751068412)
XLA Ops:
  0.0 54.9 %shard_map.73 = f32[512,256]{1,0:T(8,128)S(1)} custom-call(f32[512,256]{1,0:T(8,128)} %v0_hbm.1, f32[512,256]{1,0:T(8,128)} %src_hbm.1, f32[4,8,128,128]{3,2,1,0:T(8,128)} %et_hbm.1, f32[4,8,128,128]{3,2,1,0:T(8,128)} %it_hbm.1, s32[4,8]{1,0:T(4,128)} %ec_hbm.1, s32[4,8]{1,0:T(4,128)} %ic_hbm.1, s32[8,48]{1,0:T(8,128)} %send_hbm.1), custom_call_target="tpu_custom_call" | custom-call | tf_op jit(solution)/shard_map/pallas_call | solution.py:259
  54.9 0.8 %copy.9 = f32[512,256]{1,0:T(8,128)} copy(f32[512,256]{1,0:T(8,128)S(1)} %shard_map.73) | data formatting | bytes 1048576

commit v5 on v4

--- a/solution.py
+++ b/solution.py
@@ -97,8 +97,8 @@
             pltpu.make_async_remote_copy(
                 src_ref=pay.at[exchange, group, pl.ds(o * run, run)],
                 dst_ref=halo.at[exchange, group, pl.ds(o * run, run)],
-                send_sem=send_sem.at[exchange, group, o],
-                recv_sem=recv_sem.at[exchange, group, o],
+                send_sem=send_sem.at[exchange],
+                recv_sem=recv_sem.at[exchange % 2, group],
                 device_id=(targets[o],),
                 device_id_type=MESH,
             )
@@ -210,8 +210,8 @@
     def stage(exchange, which, half, last):
         for q in range(2):
             group = 2 * half + q
-            for copy in copies(exchange, group):
-                copy.wait_recv()
+            arrived = halo.at[exchange, group]
+            pltpu.make_async_copy(arrived, arrived, recv_sem.at[exchange % 2, group]).wait()
             left, right = [
                 jnp.concatenate(split2(x), axis=1) for x in unpack(halo[exchange, group])
             ]
@@ -242,9 +242,8 @@
             stage(exchange, exchange % 2, half, exchange == exchanges - 1)
 
     for exchange in range(exchanges):
-        for group in range(2 * halves):
-            for copy in copies(exchange, group):
-                copy.wait_send()
+        sent = pay.at[exchange]
+        pltpu.make_async_copy(sent, sent, send_sem.at[exchange]).wait()
 
 
 def on_device(devices, v0, source, et, it, ec, ic, send):
@@ -279,8 +278,8 @@
             pltpu.VMEM((2 * halves, listed // 2, LANES), F32),
             pltpu.VMEM((halves, listed, LANES), F32),
             pltpu.SemaphoreType.DMA((7,)),
-            pltpu.SemaphoreType.DMA((exchanges, 2 * halves, partners)),
-            pltpu.SemaphoreType.DMA((exchanges, 2 * halves, partners)),
+            pltpu.SemaphoreType.DMA((exchanges,)),
+            pltpu.SemaphoreType.DMA((2, 2 * halves)),
         ],
         compiler_params=pltpu.CompilerParams(
             collective_id=0, has_side_effects=True, vmem_limit_bytes=48 * 1024 * 1024

time: 55.8 us -> 52.2 us (0.935)
  Pallas kernels: 54.9 us -> 51.3 us
    pallas_call x1, Pallas kernels: 54.9 us -> 51.3 us  [on_device(): pl.pallas_call(functools.partial(kernel, devices), out_shape=jax.ShapeDty...]
where the time goes in v5:
time: 52.2 us; the launch traced here: 52.1 us
  Pallas kernels  51.3 us (98%)
  local copies, waits for them, and re-layouts  0.8 us (2%)
    pallas_call x1, Pallas kernels, on_device(): pl.pallas_call(functools.partial(kernel, devices), out_shape=jax.ShapeDty...  51.3 us

profile of v5, /device:TPU:1, one launch (start us, length us, event | category | flops | bytes accessed | tf_op | source)
XLA Modules:
  0.0 52.1 jit_solution(13301661778534602548)
XLA Ops:
  0.0 51.3 %shard_map.73 = f32[512,256]{1,0:T(8,128)S(1)} custom-call(f32[512,256]{1,0:T(8,128)} %v0_hbm.1, f32[512,256]{1,0:T(8,128)} %src_hbm.1, f32[4,8,128,128]{3,2,1,0:T(8,128)} %et_hbm.1, f32[4,8,128,128]{3,2,1,0:T(8,128)} %it_hbm.1, s32[4,8]{1,0:T(4,128)} %ec_hbm.1, s32[4,8]{1,0:T(4,128)} %ic_hbm.1, s32[8,48]{1,0:T(8,128)} %send_hbm.1), custom_call_target="tpu_custom_call" | custom-call | tf_op jit(solution)/shard_map/pallas_call | solution.py:258
  51.3 0.8 %copy.9 = f32[512,256]{1,0:T(8,128)} copy(f32[512,256]{1,0:T(8,128)S(1)} %shard_map.73) | data formatting | bytes 1048576

commit v6 on v5

--- a/solution.py
+++ b/solution.py
@@ -52,6 +52,8 @@
     pick,
     w_hi,
     w_lo,
+    u_hi,
+    u_lo,
     pay,
     halo,
     vcat,
@@ -177,8 +179,11 @@
                 rows = slice(listed + g * size, listed + (g + 1) * size)
                 w_hi[which, rows, c * size : (c + 1) * size] = hi
                 w_lo[which, rows, c * size : (c + 1) * size] = lo
-        for w in (w_hi, w_lo):
-            w[which, 0:listed] = dot(pick[...], w[which, listed:]).astype(BF16)
+        for w, u in ((w_hi, u_hi), (w_lo, u_lo)):
+            top = dot(pick[...], w[which, listed:]).astype(BF16)
+            w[which, 0:listed, 0:own] = top[:, 0:own]
+            u[which, :, 0:listed] = top[0:packed, own:]
+            u[which, :, listed:] = top[packed:, own:]
 
     loads[2].wait()
     loads[3].wait()
@@ -187,59 +192,73 @@
     for half in range(halves):
         psrc[half] = picked(src[:, half * LANES : (half + 1) * LANES])
 
-    def own_part(which, half, state, exchange, with_source):
+    def source_of(half):
+        return src[:, half * LANES : (half + 1) * LANES]
+
+    def settle(half, state, add_source):
         hi, lo = split2(state)
         vcat[half, :, 0:LANES] = hi
         vcat[half, :, LANES:] = lo
-        near = product(w_hi[which, :, 0:own], w_lo[which, :, 0:own], vcat[half])
-        head, body = near[0:listed], state + near[listed:]
-        if with_source:
-            head = head + psrc[half]
-            body = body + src[:, half * LANES : (half + 1) * LANES]
-        groups = pack(head)
+        vpart[half] = state + source_of(half) if add_source else state
+
+    def near_head(which, half, exchange, add_source):
+        head = product(w_hi[which, 0:listed, 0:own], w_lo[which, 0:listed, 0:own], vcat[half])
+        groups = pack(head + psrc[half] if add_source else head)
         for q in range(2):
             part[2 * half + q] = pay[exchange, 2 * half + q] + groups[q]
-        vpart[half] = body
+
+    def near_body(which, half):
+        vpart[half] = vpart[half] + product(
+            w_hi[which, listed:, 0:own], w_lo[which, listed:, 0:own], vcat[half]
+        )
 
     for half in range(halves):
-        own_part(0, half, v0[:, half * LANES : (half + 1) * LANES], 0, True)
+        settle(half, v0[:, half * LANES : (half + 1) * LANES], True)
+        near_head(0, half, 0, True)
+        near_body(0, half)
     loads[5].wait()
     loads[6].wait()
     build(1)
 
-    def stage(exchange, which, half, last):
-        for q in range(2):
-            group = 2 * half + q
-            arrived = halo.at[exchange, group]
-            pltpu.make_async_copy(arrived, arrived, recv_sem.at[exchange % 2, group]).wait()
-            left, right = [
-                jnp.concatenate(split2(x), axis=1) for x in unpack(halo[exchange, group])
-            ]
-            if not last:
-                payload = part[group]
-                wide = dot(w_hi[which, 0:packed, own:], left)
-                wide = wide + dot(w_hi[which, packed:listed, own:], right)
-                low = dot(w_lo[which, 0:packed, own:], left[:, :LANES])
-                low = low + dot(w_lo[which, packed:listed, own:], right[:, :LANES])
-                pay[exchange + 1, group] = payload + (
-                    (wide[:, :LANES] + wide[:, LANES:]) + low
-                )
-                send(exchange + 1, group)
-            if q == 0:
-                hcat[...] = left
-            else:
-                hcat[...] = hcat[...] + right
-        state = vpart[half] + product(
+    def urgent(exchange, which, group, last):
+        arrived = halo.at[exchange, group]
+        pltpu.make_async_copy(arrived, arrived, recv_sem.at[exchange % 2, group]).wait()
+        left, right = [jnp.concatenate(split2(x), axis=1) for x in unpack(arrived[...])]
+        if not last:
+            both = jnp.concatenate([left, right], axis=0)
+            wide = dot(u_hi[which], both)
+            low = dot(u_lo[which], both[:, :LANES])
+            pay[exchange + 1, group] = part[group] + ((wide[:, :LANES] + wide[:, LANES:]) + low)
+            send(exchange + 1, group)
+        if group % 2 == 0:
+            hcat[...] = left
+        else:
+            hcat[...] = hcat[...] + right
+
+    def far_body(which, half):
+        return vpart[half] + product(
             w_hi[which, listed:, own:], w_lo[which, listed:, own:], hcat[...]
         )
-        if last:
-            out_ref[:, half * LANES : (half + 1) * LANES] = state
-        else:
-            own_part(1 - which, half, state, exchange + 1, which == 1)
-
+
+    waiting = []
     for exchange in range(exchanges):
-        for half in range(halves):
-            stage(exchange, exchange % 2, half, exchange == exchanges - 1)
+        which = exchange % 2
+        last = exchange == exchanges - 1
+        for group in range(2 * halves):
+            urgent(exchange, which, group, last)
+            if waiting:
+                waiting.pop(0)()
+            if group % 2 == 1:
+                half = group // 2
+                state = far_body(which, half)
+                if last:
+                    out_ref[:, half * LANES : (half + 1) * LANES] = state
+                    continue
+                settle(half, state, which == 1)
+                waiting.append(
+                    functools.partial(near_head, 1 - which, half, exchange + 1, which == 1)
+                )
+                waiting.append(functools.partial(near_body, 1 - which, half))
 
     for exchange in range(exchanges):
         sent = pay.at[exchange]
@@ -270,6 +289,8 @@
             pltpu.VMEM((listed, own), BF16),
             pltpu.VMEM((2, extended, extended), BF16),
             pltpu.VMEM((2, extended, extended), BF16),
+            pltpu.VMEM((2, listed // 2, 2 * listed), BF16),
+            pltpu.VMEM((2, listed // 2, 2 * listed), BF16),
             pltpu.VMEM((exchanges, 2 * halves, listed // 2, LANES), F32),
             pltpu.VMEM((exchanges, 2 * halves, listed // 2, LANES), F32),
             pltpu.VMEM((halves, own, 2 * LANES), BF16),

time: 52.2 us -> 51.1 us (0.979)
  Pallas kernels: 51.3 us -> 50.2 us
    pallas_call x1, Pallas kernels: 51.3 us -> 50.2 us  [on_device(): pl.pallas_call(functools.partial(kernel, devices), out_shape=jax.ShapeDty...]
where the time goes in v6:
time: 51.1 us; the launch traced here: 51 us
  Pallas kernels  50.2 us (98%)
  local copies, waits for them, and re-layouts  0.8 us (2%)
    pallas_call x1, Pallas kernels, on_device(): pl.pallas_call(functools.partial(kernel, devices), out_shape=jax.ShapeDty...  50.2 us

profile of v6, /device:TPU:1, one launch (start us, length us, event | category | flops | bytes accessed | tf_op | source)
XLA Modules:
  0.0 51.0 jit_solution(7622259647851567888)
XLA Ops:
  0.0 50.2 %shard_map.73 = f32[512,256]{1,0:T(8,128)S(1)} custom-call(f32[512,256]{1,0:T(8,128)} %v0_hbm.1, f32[512,256]{1,0:T(8,128)} %src_hbm.1, f32[4,8,128,128]{3,2,1,0:T(8,128)} %et_hbm.1, f32[4,8,128,128]{3,2,1,0:T(8,128)} %it_hbm.1, s32[4,8]{1,0:T(4,128)} %ec_hbm.1, s32[4,8]{1,0:T(4,128)} %ic_hbm.1, s32[8,48]{1,0:T(8,128)} %send_hbm.1), custom_call_target="tpu_custom_call" | custom-call | tf_op jit(solution)/shard_map/pallas_call | solution.py:277
  50.2 0.8 %copy.9 = f32[512,256]{1,0:T(8,128)} copy(f32[512,256]{1,0:T(8,128)S(1)} %shard_map.73) | data formatting | bytes 1048576

commit v7 on v6

--- a/solution.py
+++ b/solution.py
@@ -12,10 +12,6 @@
 MESH = pl.DeviceIdType.MESH
 F32 = jnp.float32
 BF16 = jnp.bfloat16
-
-
-def partner_offset(offset_index):
-    return (offset_index // 2 + 1) * (1 if offset_index % 2 == 0 else -1)
 
 
 def split2(x):
@@ -76,7 +72,15 @@
     run = per_list // 2
 
     me = lax.axis_index("rows")
-    targets = [lax.rem(me + partner_offset(o) + devices, devices) for o in range(partners)]
+    core = lax.rem(me, 2)
+    reach = [4 * (p // 2 % (partners // 4)) // 2 + 1 for p in range(partners)]
+    late = [core if p < partners // 2 else 1 - core for p in range(partners)]
+    reach = [reach[p] + 1 - late[p] for p in range(partners)]
+    list_at = [2 * (reach[p] - 1) + p % 2 for p in range(partners)]
+    targets = [
+        lax.rem(me + (reach[p] if p % 2 == 0 else devices - reach[p]), devices)
+        for p in range(partners)
+    ]
 
     barrier = pltpu.get_barrier_semaphore()
     for target in targets:
@@ -94,39 +98,27 @@
     for load in loads:
         load.start()
 
-    def copies(exchange, group):
-        return [
+    def send(exchange, group, first, last):
+        for p in range(first, last):
             pltpu.make_async_remote_copy(
-                src_ref=pay.at[exchange, group, pl.ds(o * run, run)],
-                dst_ref=halo.at[exchange, group, pl.ds(o * run, run)],
+                src_ref=pay.at[exchange, group, pl.ds(p * run, run)],
+                dst_ref=halo.at[exchange, group, pl.ds(pl.multiple_of(list_at[p] * run, 8), run)],
                 send_sem=send_sem.at[exchange],
                 recv_sem=recv_sem.at[exchange % 2, group],
-                device_id=(targets[o],),
+                device_id=(targets[p],),
                 device_id_type=MESH,
-            )
-            for o in range(partners)
-        ]
-
-    def send(exchange, group):
-        ready = copies(exchange, group)
-        near = sorted(range(partners), key=lambda o: abs(partner_offset(o)))
-        for core in range(2):
-            order = sorted(near, key=lambda o: (partner_offset(o) + core) % 2)
-
-            @pl.when(lax.rem(me, 2) == core)
-            def _():
-                for o in order:
-                    ready[o].start()
+            ).start()
 
     square[...] = jnp.zeros_like(square)
     loads[0].wait()
-    square[0:partners, 0:per_list] = send_v[...].astype(F32)
+    for p in range(partners):
+        square[p : p + 1, 0:per_list] = send_v[pl.ds(list_at[p], 1), :].astype(F32)
     turned = square[...].T
     column = jnp.concatenate(
         [
-            jnp.broadcast_to(turned[part_at * run : (part_at + 1) * run, o : o + 1], (run, LANES))
+            jnp.broadcast_to(turned[part_at * run : (part_at + 1) * run, p : p + 1], (run, LANES))
             for part_at in range(2)
-            for o in range(partners)
+            for p in range(partners)
         ],
         axis=0,
     )
@@ -165,7 +157,7 @@
             pay[0, 2 * half + q] = groups[q]
             if half == 0 and q == 0:
                 pl.semaphore_wait(barrier, partners)
-            send(0, 2 * half + q)
+            send(0, 2 * half + q, 0, partners)
 
     def build(which):
         for g in range(blocks):
@@ -226,10 +218,14 @@
         left, right = [jnp.concatenate(split2(x), axis=1) for x in unpack(arrived[...])]
         if not last:
             both = jnp.concatenate([left, right], axis=0)
-            wide = dot(u_hi[which], both)
-            low = dot(u_lo[which], both[:, :LANES])
-            pay[exchange + 1, group] = part[group] + ((wide[:, :LANES] + wide[:, LANES:]) + low)
-            send(exchange + 1, group)
+            for chunk in range(2):
+                rows = slice(chunk * packed // 2, (chunk + 1) * packed // 2)
+                pay[exchange + 1, group, rows] = part[group, rows] + product(
+                    u_hi[which, rows], u_lo[which, rows], both
+                )
+                send(
+                    exchange + 1, group, chunk * partners // 2, (chunk + 1) * partners // 2
+                )
         if group % 2 == 0:
             hcat[...] = left
         else:
@@ -255,9 +251,10 @@
                     out_ref[:, half * LANES : (half + 1) * LANES] = state
                     continue
                 settle(half, state, which == 1)
-                waiting.append(
-                    functools.partial(near_head, 1 - which, half, exchange + 1, which == 1)
-                )
+                if exchange + 2 < exchanges:
+                    waiting.append(
+                        functools.partial(near_head, 1 - which, half, exchange + 1, which == 1)
+                    )
                 waiting.append(functools.partial(near_body, 1 - which, half))
 
     for exchange in range(exchanges):

time: 51.1 us -> 51.2 us (level)
  no operation moved by 1% of the time
where the time goes in v7:
time: 51.2 us; the launch traced here: 51.1 us
  Pallas kernels  50.3 us (98%)
  local copies, waits for them, and re-layouts  0.8 us (2%)
    pallas_call x1, Pallas kernels, on_device(): pl.pallas_call(functools.partial(kernel, devices), out_shape=jax.ShapeDty...  50.3 us

profile of v7, /device:TPU:1, one launch (start us, length us, event | category | flops | bytes accessed | tf_op | source)
XLA Modules:
  0.0 51.1 jit_solution(15100121883489591787)
XLA Ops:
  0.0 50.3 %shard_map.73 = f32[512,256]{1,0:T(8,128)S(1)} custom-call(f32[512,256]{1,0:T(8,128)} %v0_hbm.1, f32[512,256]{1,0:T(8,128)} %src_hbm.1, f32[4,8,128,128]{3,2,1,0:T(8,128)} %et_hbm.1, f32[4,8,128,128]{3,2,1,0:T(8,128)} %it_hbm.1, s32[4,8]{1,0:T(4,128)} %ec_hbm.1, s32[4,8]{1,0:T(4,128)} %ic_hbm.1, s32[8,48]{1,0:T(8,128)} %send_hbm.1), custom_call_target="tpu_custom_call" | custom-call | tf_op jit(solution)/shard_map/pallas_call | solution.py:274
  50.3 0.8 %copy.9 = f32[512,256]{1,0:T(8,128)} copy(f32[512,256]{1,0:T(8,128)S(1)} %shard_map.73) | data formatting | bytes 1048576

commit v8 on v7

--- a/solution.py
+++ b/solution.py
@@ -46,6 +46,7 @@
     send_v,
     square,
     pick,
+    move,
     w_hi,
     w_lo,
     u_hi,
@@ -98,8 +99,8 @@
     for load in loads:
         load.start()
 
-    def send(exchange, group, first, last):
-        for p in range(first, last):
+    def send(exchange, group):
+        for p in range(partners):
             pltpu.make_async_remote_copy(
                 src_ref=pay.at[exchange, group, pl.ds(p * run, run)],
                 dst_ref=halo.at[exchange, group, pl.ds(pl.multiple_of(list_at[p] * run, 8), run)],
@@ -139,10 +140,22 @@
 
     def unpack(x):
         turned_x = turn(x)
-        lists = (partners, run, LANES)
-        left = [jnp.where(first, y, 0.0).reshape(lists) for y in (x, turned_x)]
-        right = [jnp.where(first, 0.0, y).reshape(lists) for y in (turned_x, x)]
-        return [jnp.concatenate(y, axis=1).reshape(listed, LANES) for y in (left, right)]
+        direct = jnp.concatenate([jnp.where(first, x, 0.0), jnp.where(first, 0.0, x)], axis=0)
+        other = jnp.concatenate(
+            [jnp.where(first, 0.0, turned_x), jnp.where(first, turned_x, 0.0)], axis=0
+        )
+        return direct, other
+
+    across = lax.broadcasted_iota(jnp.int32, (run, listed), 1)
+    down = lax.broadcasted_iota(jnp.int32, (run, listed), 0)
+    move[...] = jnp.concatenate(
+        [
+            jnp.where(across == down + (part_at * packed + o * run), 1.0, 0.0)
+            for o in range(partners)
+            for part_at in range(2)
+        ],
+        axis=0,
+    ).astype(BF16)
 
     def picked(x):
         hi, mid = split2(x)
@@ -157,7 +170,7 @@
             pay[0, 2 * half + q] = groups[q]
             if half == 0 and q == 0:
                 pl.semaphore_wait(barrier, partners)
-            send(0, 2 * half + q, 0, partners)
+            send(0, 2 * half + q)
 
     def build(which):
         for g in range(blocks):
@@ -172,10 +185,13 @@
                 w_hi[which, rows, c * size : (c + 1) * size] = hi
                 w_lo[which, rows, c * size : (c + 1) * size] = lo
         for w, u in ((w_hi, u_hi), (w_lo, u_lo)):
-            top = dot(pick[...], w[which, listed:]).astype(BF16)
-            w[which, 0:listed, 0:own] = top[:, 0:own]
-            u[which, :, 0:listed] = top[0:packed, own:]
-            u[which, :, listed:] = top[packed:, own:]
+            w[which, listed:, own:] = dot(w[which, listed:, own:], move[...]).astype(BF16)
+            top = dot(pick[...], w[which, listed:])
+            w[which, 0:listed, 0:own] = top[:, 0:own].astype(BF16)
+            one, two = top[0:packed, own:], top[packed:, own:]
+            in_one = lax.broadcasted_iota(jnp.int32, (packed, listed), 1) < packed
+            u[which, :, 0:listed] = jnp.where(in_one, one, two).astype(BF16)
+            u[which, :, listed:] = jnp.where(in_one, two, one).astype(BF16)
 
     loads[2].wait()
     loads[3].wait()
@@ -215,21 +231,15 @@
     def urgent(exchange, which, group, last):
         arrived = halo.at[exchange, group]
         pltpu.make_async_copy(arrived, arrived, recv_sem.at[exchange % 2, group]).wait()
-        left, right = [jnp.concatenate(split2(x), axis=1) for x in unpack(arrived[...])]
+        direct, other = [jnp.concatenate(split2(x), axis=1) for x in unpack(arrived[...])]
         if not last:
-            both = jnp.concatenate([left, right], axis=0)
-            for chunk in range(2):
-                rows = slice(chunk * packed // 2, (chunk + 1) * packed // 2)
-                pay[exchange + 1, group, rows] = part[group, rows] + product(
-                    u_hi[which, rows], u_lo[which, rows], both
-                )
-                send(
-                    exchange + 1, group, chunk * partners // 2, (chunk + 1) * partners // 2
-                )
+            both = jnp.concatenate([direct, other], axis=0)
+            pay[exchange + 1, group] = part[group] + product(u_hi[which], u_lo[which], both)
+            send(exchange + 1, group)
         if group % 2 == 0:
-            hcat[...] = left
+            hcat[...] = jnp.concatenate([direct[0:packed], other[packed:]], axis=0)
         else:
-            hcat[...] = hcat[...] + right
+            hcat[...] += jnp.concatenate([other[0:packed], direct[packed:]], axis=0)
 
     def far_body(which, half):
         return vpart[half] + product(
@@ -284,6 +294,7 @@
             pltpu.VMEM((partners, per_list), jnp.int32),
             pltpu.VMEM((LANES, LANES), F32),
             pltpu.VMEM((listed, own), BF16),
+            pltpu.VMEM((listed, listed), BF16),
             pltpu.VMEM((2, extended, extended), BF16),
             pltpu.VMEM((2, extended, extended), BF16),
             pltpu.VMEM((2, listed // 2, 2 * listed), BF16),

time: 51.2 us -> 51.1 us (level)
  no operation moved by 1% of the time
where the time goes in v8:
time: 51.1 us; the launch traced here: 51 us
  Pallas kernels  50.2 us (98%)
  local copies, waits for them, and re-layouts  0.8 us (2%)
    pallas_call x1, Pallas kernels, on_device(): pl.pallas_call(functools.partial(kernel, devices), out_shape=jax.ShapeDty...  50.2 us

profile of v8, /device:TPU:1, one launch (start us, length us, event | category | flops | bytes accessed | tf_op | source)
XLA Modules:
  0.0 51.0 jit_solution(640670953158483533)
XLA Ops:
  0.0 50.2 %shard_map.73 = f32[512,256]{1,0:T(8,128)S(1)} custom-call(f32[512,256]{1,0:T(8,128)} %v0_hbm.1, f32[512,256]{1,0:T(8,128)} %src_hbm.1, f32[4,8,128,128]{3,2,1,0:T(8,128)} %et_hbm.1, f32[4,8,128,128]{3,2,1,0:T(8,128)} %it_hbm.1, s32[4,8]{1,0:T(4,128)} %ec_hbm.1, s32[4,8]{1,0:T(4,128)} %ic_hbm.1, s32[8,48]{1,0:T(8,128)} %send_hbm.1), custom_call_target="tpu_custom_call" | custom-call | tf_op jit(solution)/shard_map/pallas_call | solution.py:284
  50.2 0.8 %copy.9 = f32[512,256]{1,0:T(8,128)} copy(f32[512,256]{1,0:T(8,128)S(1)} %shard_map.73) | data formatting | bytes 1048576
